TPU v7x, 256 devices: a whole 4x4x8 slice. The times are simulated.
256 devices in a mesh: lon: 4 (over y), lat: 4 (over x), mem: 16 (over z, core).
Axes of the slice: x: 4, y: 4, z: 8, core: 2. Of those that a mesh axis runs over, the one named last changes fastest.
Arguments:
- north_vel: bfloat16 [16, 4, 75, 128, 512], P('mem', None, None, 'lat', 'lon'), may hold values from -6 to 6
- up_vel: bfloat16 [16, 4, 75, 128, 512], P('mem', None, None, 'lat', 'lon'), may hold values from -6 to 6
- dens_class: int32 [16, 4, 75, 128, 512], P('mem', None, None, 'lat', 'lon'), may hold values from 0 to 79
- thickness: int32 [75, 128, 512], P(None, 'lat', 'lon'), may hold values from 0 to 2000
- basin_id: int32 [128, 512], P('lat', 'lon'), may hold values from 0 to 3
Outputs:
- depth_mean: float32 [4, 4, 2, 75, 128], P('lon', None, None, None, 'lat')
- depth_spread: float32 [4, 4, 2, 75, 128], P('lon', None, None, None, 'lat')
- class_mean: float32 [4, 4, 2, 80, 128], P('lon', None, None, None, 'lat')
- class_spread: float32 [4, 4, 2, 80, 128], P('lon', None, None, None, 'lat')
Inputs may be any that keep to these rules, and one draw needn't show every extreme that they name: `basin_id`: 0 marks land; 1 to 3 name the basins. `thickness`: thousandths of a unit layer; 0 marks a cell below the sea floor.
All inputs are finite; a program needn't handle non-finite values.
Results may differ from a plain program's by a relative error of at most 0.0029.
Values sent between devices are 32-bit elements; how exact they have to be, the bound alone decides.
A program may use at most 128 MiB of HBM per device.

v0:
```python
import math

import jax
import jax.numpy as jnp
from jax import lax
from jax.sharding import PartitionSpec as P

CLASSES = 80
BASINS = 3


north_unit = 0.02
up_unit = 0.01


def cut_along(shard, dim, devices):
    dims = shard.shape
    parts = shard.reshape(*dims[:dim], devices, dims[dim] // devices, *dims[dim + 1 :])
    return jnp.moveaxis(parts, dim, 0)


def summed_on_arrival(shard, axis, dim):
    devices = lax.axis_size(axis)
    parts = lax.all_to_all(cut_along(shard, dim, devices), axis, 0, 0, tiled=True)
    return jnp.sum(parts, axis=0)


def in_one_piece(arrays, axis, dim, along):
    ends, at = ([], 0)
    for a in arrays[:-1]:
        at += a.shape[along]
        ends.append(at)
    both = jnp.concatenate(arrays, axis=along)
    return tuple(jnp.split(summed_on_arrival(both, axis, dim), ends, axis=along))


def in_one_piece_2(arrays, axis, dim, along):
    ends, at = ([], 0)
    for a in arrays[:-1]:
        at += a.shape[along]
        ends.append(at)
    both = jnp.concatenate(arrays, axis=along)
    return tuple(jnp.split(lax.all_gather(both, axis, axis=dim, tiled=True), ends, axis=along))


def filled_up(lines, devices):
    spare = -lines.shape[0] % devices
    if not spare:
        return lines
    return jnp.concatenate([lines, jnp.zeros((spare, *lines.shape[1:]), lines.dtype)])


def sent_to_all(shard, axis):
    copies = jnp.broadcast_to(shard, (lax.axis_size(axis), *shard.shape))
    return lax.all_to_all(copies, axis, split_axis=0, concat_axis=0, tiled=True)


def in_order(parts, dim):
    parts = jnp.moveaxis(parts, 0, dim)
    dims = parts.shape
    return parts.reshape(*dims[:dim], dims[dim] * dims[dim + 1], *dims[dim + 2 :])


def gather_directly(shard, axis, dim):
    parts = sent_to_all(shard, axis)
    return in_order(parts, dim)


def nested_sum(shard, axes):
    padded = filled_up(shard, lax.axis_size(axes))
    whole = gather_directly(summed_on_arrival(padded, axes, 0), axes, 0)
    return lax.slice_in_dim(whole, 0, len(shard)).reshape(shard.shape)


def packed_total(arrays, axis):
    ends = [0]
    for a in arrays:
        ends.append(ends[-1] + a.size)
    subtotal = nested_sum(jnp.concatenate([a.ravel() for a in arrays]), axis)
    return tuple((subtotal[b:e].reshape(a.shape) for a, b, e in zip(arrays, ends, ends[1:])))


def class_sums(north_flux, rise_flux, dens_class, basin_id):
    months, levels, lat_rows, lon_cells = north_flux.shape
    block = 1
    for cand in range(16, 0, -1):
        if levels % cand == 0:
            block = cand
            break
    turns = months * (levels // block)
    weighted = jnp.stack([north_flux, rise_flux], 1).reshape(
        months, 2, levels // block, block, lat_rows, lon_cells
    )
    weighted = jnp.moveaxis(weighted, 2, 1).reshape(turns, 2, block, lat_rows, lon_cells)
    combined = jnp.where(
        basin_id[None, None] > 0, (basin_id[None, None] - 1) * CLASSES + dens_class, -1
    )
    combined = combined.reshape(turns, block, lat_rows, lon_cells)
    column_ids = jnp.arange(BASINS * CLASSES, dtype=jnp.int32)

    def one_block(packed):
        onehot = (packed[1][..., None] == column_ids).astype(jnp.bfloat16)
        return jnp.einsum("skji,kjiq->sqj", packed[0], onehot, preferred_element_type=jnp.float32)

    per_block = lax.map(one_block, (weighted, combined))
    per_block = per_block.reshape(months, levels // block, 2, BASINS, CLASSES, lat_rows)
    return jnp.swapaxes(jnp.sum(per_block, axis=1), 1, 2)


def local_tables(north_vel, up_vel, dens_class, thickness, basin_id, first_row, lat_total):
    months, levels, lat_rows, lon_cells = north_vel.shape
    row_index = first_row + jnp.arange(lat_rows, dtype=jnp.int32)
    latitude = (-78.0 + 156.0 * (row_index.astype(jnp.float32) + 0.5) / lat_total) * (
        math.pi / 180.0
    )
    zonal_width = jnp.cos(latitude)
    layer_depth = thickness.astype(jnp.float32) * 0.001
    wet_cells = (thickness > 0).astype(jnp.float32)
    north_flux = (
        north_vel.astype(jnp.float32)
        * (north_unit * zonal_width)[None, None, :, None]
        * layer_depth[None]
    ).astype(jnp.bfloat16)
    rise_flux = (
        up_vel.astype(jnp.float32) * (up_unit * zonal_width)[None, None, :, None] * wet_cells[None]
    ).astype(jnp.bfloat16)
    basin_masks = (
        basin_id[None] == jnp.arange(1, BASINS + 1, dtype=jnp.int32)[:, None, None]
    ).astype(jnp.bfloat16)
    north_depth = jnp.einsum(
        "mkji,bji->mbkj", north_flux, basin_masks, preferred_element_type=jnp.float32
    )
    rise_depth = jnp.einsum(
        "mkji,bji->mbkj", rise_flux, basin_masks, preferred_element_type=jnp.float32
    )
    depth_tab = jnp.stack([north_depth, rise_depth], 2)
    class_tab = class_sums(north_flux, rise_flux, dens_class, basin_id)
    return (class_tab, depth_tab)


def with_global(tables):
    return jnp.concatenate([jnp.sum(tables, axis=2, keepdims=True), tables], 2)


def body(north_vel, up_vel, dens_class, thickness, basin_id):
    row_count = north_vel.shape[3]
    first_row = lax.axis_index("lat") * row_count
    lat_total = row_count * lax.axis_size("lat")

    def one_member(packed):
        return local_tables(
            packed[0], packed[1], packed[2], thickness, basin_id, first_row, lat_total
        )

    class_tab, depth_tab = lax.map(one_member, (north_vel, up_vel, dens_class))
    class_tab, depth_tab = in_one_piece((class_tab, depth_tab), "lon", 1, 4)
    class_reg = with_global(class_tab)
    depth_reg = with_global(depth_tab)
    class_block = jnp.sum(class_reg[:, :, :, 1], axis=-1)
    depth_block = jnp.sum(depth_reg[:, :, :, 1], axis=-1)
    all_class, all_depth = in_one_piece_2((class_block[None], depth_block[None]), "lat", 0, 4)
    below_mask = (jnp.arange(all_class.shape[0], dtype=jnp.int32) < lax.axis_index("lat")).astype(
        jnp.float32
    )
    carry_class = jnp.sum(all_class * below_mask[:, None, None, None, None], axis=0)
    carry_depth = jnp.sum(all_depth * below_mask[:, None, None, None, None], axis=0)
    class_south = jnp.cumsum(class_reg[:, :, :, 1], axis=4) + carry_class[..., None]
    class_moc = jnp.stack(
        [jnp.cumsum(class_reg[:, :, :, 0], axis=3), jnp.cumsum(class_south, axis=3)], 3
    )
    depth_south = jnp.cumsum(depth_reg[:, :, :, 1], axis=4) + carry_depth[..., None]
    depth_moc = jnp.stack([jnp.cumsum(depth_reg[:, :, :, 0], axis=3), depth_south], 3)
    members = class_moc.shape[0] * lax.axis_size("mem")
    class_total, depth_total, class_square, depth_square = packed_total(
        (
            jnp.sum(class_moc, 0),
            jnp.sum(depth_moc, 0),
            jnp.sum(jnp.square(class_moc), 0),
            jnp.sum(jnp.square(depth_moc), 0),
        ),
        "mem",
    )
    class_mean = class_total / members
    depth_mean = depth_total / members
    class_spread = jnp.sqrt(
        jnp.maximum((class_square - class_total * class_mean) / (members - 1), 0.0)
    )
    depth_spread = jnp.sqrt(
        jnp.maximum((depth_square - depth_total * depth_mean) / (members - 1), 0.0)
    )
    return (depth_mean, depth_spread, class_mean, class_spread)


def solution(mesh):
    in_specs = (
        P("mem", None, None, "lat", "lon"),
        P("mem", None, None, "lat", "lon"),
        P("mem", None, None, "lat", "lon"),
        P(None, "lat", "lon"),
        P("lat", "lon"),
    )
    out_specs = (
        P("lon", None, None, None, "lat"),
        P("lon", None, None, None, "lat"),
        P("lon", None, None, None, "lat"),
        P("lon", None, None, None, "lat"),
    )
    return jax.shard_map(body, mesh=mesh, in_specs=in_specs, out_specs=out_specs, check_vma=False)
```

profile of v0, /device:TPU:1, one launch (start us, length us, event | category | flops | bytes accessed | tf_op | source)
XLA Modules:
  0.0 360.9 jit_solution(4421854090165047260)
XLA Ops:
  21.3 252.0 %while.19 = (s32[]{:T(128)}, f32[20,2,240,32]{2,3,1,0:T(8,128)S(1)}, s32[20,15,32,128]{3,2,1,0:T(8,128)}, bf16[20,2,15,32,128]{4,3,2,1,0:T(8,128)(2,1)}, s32[]{:T(128)}) while((s32[]{:T(128)}, f32[20,2,240,32]{2,3,1,0:T(8,128)S(1)}, s32[20,15,32,128]{3,2,1,0:T(8,128)}, bf16[20,2,15,32,128]{4,3,2,1,0:T(8,128)(2,1)}, s32[]{:T(128)}) %tuple.49), condition=%wide.region_1.2_spmd.clone, body=%wide.region_0.1_spmd.clone.sunk | while | flops 73728000 | bytes 2158665 | solution.py:105
  23.4 10.5 %fusion.54 = f32[1,2,240,32]{2,1,3,0:T(2,128)S(1)} fusion(s32[15,32,128]{2,0,1:T(8,128)S(1)} %bitcast.89, bf16[1,2,15,32,128]{4,3,2,1,0:T(8,128)(2,1)S(1)} %constant_dynamic-slice_fusion.5), kind=kOutput, calls=%fused_computation.4.clone.1 | convolution fusion | flops 73728000 | bytes 552960 | tf_op jit(solution)/shard_map/while/body/eval_jaxpr/while/body/eval_jaxpr/skji,kjiq->sqj/dot_general | solution.py:103
  36.0 10.5 %fusion.54 = f32[1,2,240,32]{2,1,3,0:T(2,128)S(1)} fusion(s32[15,32,128]{2,0,1:T(8,128)S(1)} %bitcast.89, bf16[1,2,15,32,128]{4,3,2,1,0:T(8,128)(2,1)S(1)} %constant_dynamic-slice_fusion.5), kind=kOutput, calls=%fused_computation.4.clone.1 | convolution fusion | flops 73728000 | bytes 552960 | tf_op jit(solution)/shard_map/while/body/eval_jaxpr/while/body/eval_jaxpr/skji,kjiq->sqj/dot_general | solution.py:103
  48.6 10.5 %fusion.54 = f32[1,2,240,32]{2,1,3,0:T(2,128)S(1)} fusion(s32[15,32,128]{2,0,1:T(8,128)S(1)} %bitcast.89, bf16[1,2,15,32,128]{4,3,2,1,0:T(8,128)(2,1)S(1)} %constant_dynamic-slice_fusion.5), kind=kOutput, calls=%fused_computation.4.clone.1 | convolution fusion | flops 73728000 | bytes 552960 | tf_op jit(solution)/shard_map/while/body/eval_jaxpr/while/body/eval_jaxpr/skji,kjiq->sqj/dot_general | solution.py:103
  61.2 10.5 %fusion.54 = f32[1,2,240,32]{2,1,3,0:T(2,128)S(1)} fusion(s32[15,32,128]{2,0,1:T(8,128)S(1)} %bitcast.89, bf16[1,2,15,32,128]{4,3,2,1,0:T(8,128)(2,1)S(1)} %constant_dynamic-slice_fusion.5), kind=kOutput, calls=%fused_computation.4.clone.1 | convolution fusion | flops 73728000 | bytes 552960 | tf_op jit(solution)/shard_map/while/body/eval_jaxpr/while/body/eval_jaxpr/skji,kjiq->sqj/dot_general | solution.py:103
  73.8 10.5 %fusion.54 = f32[1,2,240,32]{2,1,3,0:T(2,128)S(1)} fusion(s32[15,32,128]{2,0,1:T(8,128)S(1)} %bitcast.89, bf16[1,2,15,32,128]{4,3,2,1,0:T(8,128)(2,1)S(1)} %constant_dynamic-slice_fusion.5), kind=kOutput, calls=%fused_computation.4.clone.1 | convolution fusion | flops 73728000 | bytes 552960 | tf_op jit(solution)/shard_map/while/body/eval_jaxpr/while/body/eval_jaxpr/skji,kjiq->sqj/dot_general | solution.py:103
  86.5 10.5 %fusion.54 = f32[1,2,240,32]{2,1,3,0:T(2,128)S(1)} fusion(s32[15,32,128]{2,0,1:T(8,128)S(1)} %bitcast.89, bf16[1,2,15,32,128]{4,3,2,1,0:T(8,128)(2,1)S(1)} %constant_dynamic-slice_fusion.5), kind=kOutput, calls=%fused_computation.4.clone.1 | convolution fusion | flops 73728000 | bytes 552960 | tf_op jit(solution)/shard_map/while/body/eval_jaxpr/while/body/eval_jaxpr/skji,kjiq->sqj/dot_general | solution.py:103
  99.1 10.5 %fusion.54 = f32[1,2,240,32]{2,1,3,0:T(2,128)S(1)} fusion(s32[15,32,128]{2,0,1:T(8,128)S(1)} %bitcast.89, bf16[1,2,15,32,128]{4,3,2,1,0:T(8,128)(2,1)S(1)} %constant_dynamic-slice_fusion.5), kind=kOutput, calls=%fused_computation.4.clone.1 | convolution fusion | flops 73728000 | bytes 552960 | tf_op jit(solution)/shard_map/while/body/eval_jaxpr/while/body/eval_jaxpr/skji,kjiq->sqj/dot_general | solution.py:103
  111.7 10.5 %fusion.54 = f32[1,2,240,32]{2,1,3,0:T(2,128)S(1)} fusion(s32[15,32,128]{2,0,1:T(8,128)S(1)} %bitcast.89, bf16[1,2,15,32,128]{4,3,2,1,0:T(8,128)(2,1)S(1)} %constant_dynamic-slice_fusion.5), kind=kOutput, calls=%fused_computation.4.clone.1 | convolution fusion | flops 73728000 | bytes 552960 | tf_op jit(solution)/shard_map/while/body/eval_jaxpr/while/body/eval_jaxpr/skji,kjiq->sqj/dot_general | solution.py:103
  124.3 10.5 %fusion.54 = f32[1,2,240,32]{2,1,3,0:T(2,128)S(1)} fusion(s32[15,32,128]{2,0,1:T(8,128)S(1)} %bitcast.89, bf16[1,2,15,32,128]{4,3,2,1,0:T(8,128)(2,1)S(1)} %constant_dynamic-slice_fusion.5), kind=kOutput, calls=%fused_computation.4.clone.1 | convolution fusion | flops 73728000 | bytes 552960 | tf_op jit(solution)/shard_map/while/body/eval_jaxpr/while/body/eval_jaxpr/skji,kjiq->sqj/dot_general | solution.py:103
  136.9 10.5 %fusion.54 = f32[1,2,240,32]{2,1,3,0:T(2,128)S(1)} fusion(s32[15,32,128]{2,0,1:T(8,128)S(1)} %bitcast.89, bf16[1,2,15,32,128]{4,3,2,1,0:T(8,128)(2,1)S(1)} %constant_dynamic-slice_fusion.5), kind=kOutput, calls=%fused_computation.4.clone.1 | convolution fusion | flops 73728000 | bytes 552960 | tf_op jit(solution)/shard_map/while/body/eval_jaxpr/while/body/eval_jaxpr/skji,kjiq->sqj/dot_general | solution.py:103
  149.5 10.5 %fusion.54 = f32[1,2,240,32]{2,1,3,0:T(2,128)S(1)} fusion(s32[15,32,128]{2,0,1:T(8,128)S(1)} %bitcast.89, bf16[1,2,15,32,128]{4,3,2,1,0:T(8,128)(2,1)S(1)} %constant_dynamic-slice_fusion.5), kind=kOutput, calls=%fused_computation.4.clone.1 | convolution fusion | flops 73728000 | bytes 552960 | tf_op jit(solution)/shard_map/while/body/eval_jaxpr/while/body/eval_jaxpr/skji,kjiq->sqj/dot_general | solution.py:103
  162.1 10.5 %fusion.54 = f32[1,2,240,32]{2,1,3,0:T(2,128)S(1)} fusion(s32[15,32,128]{2,0,1:T(8,128)S(1)} %bitcast.89, bf16[1,2,15,32,128]{4,3,2,1,0:T(8,128)(2,1)S(1)} %constant_dynamic-slice_fusion.5), kind=kOutput, calls=%fused_computation.4.clone.1 | convolution fusion | flops 73728000 | bytes 552960 | tf_op jit(solution)/shard_map/while/body/eval_jaxpr/while/body/eval_jaxpr/skji,kjiq->sqj/dot_general | solution.py:103
  174.7 10.5 %fusion.54 = f32[1,2,240,32]{2,1,3,0:T(2,128)S(1)} fusion(s32[15,32,128]{2,0,1:T(8,128)S(1)} %bitcast.89, bf16[1,2,15,32,128]{4,3,2,1,0:T(8,128)(2,1)S(1)} %constant_dynamic-slice_fusion.5), kind=kOutput, calls=%fused_computation.4.clone.1 | convolution fusion | flops 73728000 | bytes 552960 | tf_op jit(solution)/shard_map/while/body/eval_jaxpr/while/body/eval_jaxpr/skji,kjiq->sqj/dot_general | solution.py:103
  187.3 10.5 %fusion.54 = f32[1,2,240,32]{2,1,3,0:T(2,128)S(1)} fusion(s32[15,32,128]{2,0,1:T(8,128)S(1)} %bitcast.89, bf16[1,2,15,32,128]{4,3,2,1,0:T(8,128)(2,1)S(1)} %constant_dynamic-slice_fusion.5), kind=kOutput, calls=%fused_computation.4.clone.1 | convolution fusion | flops 73728000 | bytes 552960 | tf_op jit(solution)/shard_map/while/body/eval_jaxpr/while/body/eval_jaxpr/skji,kjiq->sqj/dot_general | solution.py:103
  199.9 10.5 %fusion.54 = f32[1,2,240,32]{2,1,3,0:T(2,128)S(1)} fusion(s32[15,32,128]{2,0,1:T(8,128)S(1)} %bitcast.89, bf16[1,2,15,32,128]{4,3,2,1,0:T(8,128)(2,1)S(1)} %constant_dynamic-slice_fusion.5), kind=kOutput, calls=%fused_computation.4.clone.1 | convolution fusion | flops 73728000 | bytes 552960 | tf_op jit(solution)/shard_map/while/body/eval_jaxpr/while/body/eval_jaxpr/skji,kjiq->sqj/dot_general | solution.py:103
  212.5 10.5 %fusion.54 = f32[1,2,240,32]{2,1,3,0:T(2,128)S(1)} fusion(s32[15,32,128]{2,0,1:T(8,128)S(1)} %bitcast.89, bf16[1,2,15,32,128]{4,3,2,1,0:T(8,128)(2,1)S(1)} %constant_dynamic-slice_fusion.5), kind=kOutput, calls=%fused_computation.4.clone.1 | convolution fusion | flops 73728000 | bytes 552960 | tf_op jit(solution)/shard_map/while/body/eval_jaxpr/while/body/eval_jaxpr/skji,kjiq->sqj/dot_general | solution.py:103
  225.1 10.5 %fusion.54 = f32[1,2,240,32]{2,1,3,0:T(2,128)S(1)} fusion(s32[15,32,128]{2,0,1:T(8,128)S(1)} %bitcast.89, bf16[1,2,15,32,128]{4,3,2,1,0:T(8,128)(2,1)S(1)} %constant_dynamic-slice_fusion.5), kind=kOutput, calls=%fused_computation.4.clone.1 | convolution fusion | flops 73728000 | bytes 552960 | tf_op jit(solution)/shard_map/while/body/eval_jaxpr/while/body/eval_jaxpr/skji,kjiq->sqj/dot_general | solution.py:103
  237.7 10.5 %fusion.54 = f32[1,2,240,32]{2,1,3,0:T(2,128)S(1)} fusion(s32[15,32,128]{2,0,1:T(8,128)S(1)} %bitcast.89, bf16[1,2,15,32,128]{4,3,2,1,0:T(8,128)(2,1)S(1)} %constant_dynamic-slice_fusion.5), kind=kOutput, calls=%fused_computation.4.clone.1 | convolution fusion | flops 73728000 | bytes 552960 | tf_op jit(solution)/shard_map/while/body/eval_jaxpr/while/body/eval_jaxpr/skji,kjiq->sqj/dot_general | solution.py:103
  250.3 10.5 %fusion.54 = f32[1,2,240,32]{2,1,3,0:T(2,128)S(1)} fusion(s32[15,32,128]{2,0,1:T(8,128)S(1)} %bitcast.89, bf16[1,2,15,32,128]{4,3,2,1,0:T(8,128)(2,1)S(1)} %constant_dynamic-slice_fusion.5), kind=kOutput, calls=%fused_computation.4.clone.1 | convolution fusion | flops 73728000 | bytes 552960 | tf_op jit(solution)/shard_map/while/body/eval_jaxpr/while/body/eval_jaxpr/skji,kjiq->sqj/dot_general | solution.py:103
  262.9 10.5 %fusion.54 = f32[1,2,240,32]{2,1,3,0:T(2,128)S(1)} fusion(s32[15,32,128]{2,0,1:T(8,128)S(1)} %bitcast.89, bf16[1,2,15,32,128]{4,3,2,1,0:T(8,128)(2,1)S(1)} %constant_dynamic-slice_fusion.5), kind=kOutput, calls=%fused_computation.4.clone.1 | convolution fusion | flops 73728000 | bytes 552960 | tf_op jit(solution)/shard_map/while/body/eval_jaxpr/while/body/eval_jaxpr/skji,kjiq->sqj/dot_general | solution.py:103
  299.4 10.5 %all_gather.3 = f32[4,1,1,4,155]{4,3,2,1,0:T(4,128)S(1)} all-gather(f32[1,1,1,4,155]{4,3,2,1,0:T(4,128)S(1)} %pad_maximum_fusion.6), channel_id=1, replica_groups=mesh['lon'=4,'lat'=4,'mem'=16] {'lat'}, dimensions={0}, use_global_device_ids=true | all-gather | bytes 12400 | tf_op jit(solution)/shard_map/all_gather | solution.py:43
  314.0 25.8 %all_to_all.20 = f32[16,1,4960]{2,1,0:T(1,128)S(1)} all-to-all(f32[16,1,4960]{2,1,0:T(1,128)S(1)} %all_to_all.14), channel_id=1, replica_groups=mesh['lon'=4,'lat'=4,'mem'=16] {'mem'}, dimensions={0} | all-to-all | bytes 634880 | tf_op jit(solution)/shard_map/all_to_all | solution.py:24
  340.2 15.6 %all_to_all.21 = f32[16,1,4960]{2,1,0:T(1,128)S(1)} all-to-all(f32[16,1,4960]{2,1,0:T(1,128)S(1)} %broadcast_in_dim.76), channel_id=1, replica_groups=mesh['lon'=4,'lat'=4,'mem'=16] {'mem'}, dimensions={0} | all-to-all | bytes 634880 | tf_op jit(solution)/shard_map/all_to_all | solution.py:55
  (165 shorter events, 98.0 us)
Async XLA Ops:
  0.6 1.7 copy-start.4
  0.6 1.8 copy-start.6
  2.5 2.6 copy-start.2
  5.1 2.2 copy-start.3
  15.9 5.4 %copy-start.5 = (f32[20,2,240,32]{2,3,1,0:T(8,128)S(1)}, f32[20,2,240,32]{2,3,1,0:T(8,128)}, u32[]{:S(2)}) copy-start(f32[20,2,240,32]{2,3,1,0:T(8,128)} %custom-call.1) | copy-start | bytes 3686404
  275.6 2.8 copy-start
  278.3 2.0 copy-start.1
  283.6 15.4 %all-to-all-start = ((f32[4,1,1,3,2,155,32]{5,6,4,3,2,1,0:T(8,128)}), f32[4,1,1,3,2,155,32]{5,6,4,3,2,1,0:T(8,128)S(1)}, u32[]{:S(2)}, u32[]{:S(2)}) async-start(f32[4,1,1,3,2,155,32]{5,6,4,3,2,1,0:T(8,128)} %maximum_bitcast_fusion), calls=%async_computation | async-start | bytes 1572864 | tf_op jit(solution)/shard_map/all_to_all | solution.py:24
where the time goes:
time: 362 us; the launch traced here: 361 us
  matrix products  213 us (59%)
  blocking collectives  51.9 us (14%)
  local copies, waits for them, and re-layouts  49.8 us (14%)
  other arithmetic  29 us (8%)
  waiting for transfers between devices  10.4 us (3%)
  starting transfers between devices  5 us (1%)
    dot_general x20, matrix products, one_block(): jnp.einsum('skji,kjiq->sqj', packed[0], onehot, preferred_element_type=jn...  209 us
    dynamic_slice x60, local copies, waits for them, and re-layouts, class_sums(): per_block = lax.map(one_block, (weighted, combined))  41.6 us
    all_to_all x1, blocking collectives, summed_on_arrival(): lax.all_to_all(cut_along(shard, dim, devices), axis, 0, 0, tiled=True)  25.8 us
    all_to_all x1, blocking collectives, sent_to_all(): return lax.all_to_all(copies, axis, split_axis=0, concat_axis=0, tiled=True)  15.6 us
    all_gather x1, blocking collectives, in_one_piece_2(): lax.all_gather(both, axis, axis=dim, tiled=True)  10.5 us
    all_to_all x1, waiting for transfers between devices, summed_on_arrival(): lax.all_to_all(cut_along(shard, dim, devices), axis, 0, 0, tiled=True)  10.4 us
  transfers between devices with their start and end apart: 1, of which 1 were waited for; matrix products, arithmetic and copies ran while one was open for 0% of the time, Pallas kernels for 0%

commit v1 on v0

--- a/solution.py
+++ b/solution.py
@@ -1,8 +1,11 @@
+import functools
 import math
 
 import jax
 import jax.numpy as jnp
 from jax import lax
+from jax.experimental import pallas as pl
+from jax.experimental.pallas import tpu as pltpu
 from jax.sharding import PartitionSpec as P
 
 CLASSES = 80
@@ -80,62 +83,145 @@
     return tuple((subtotal[b:e].reshape(a.shape) for a, b, e in zip(arrays, ends, ends[1:])))
 
 
-def class_sums(north_flux, rise_flux, dens_class, basin_id):
-    months, levels, lat_rows, lon_cells = north_flux.shape
-    block = 1
-    for cand in range(16, 0, -1):
-        if levels % cand == 0:
-            block = cand
-            break
-    turns = months * (levels // block)
-    weighted = jnp.stack([north_flux, rise_flux], 1).reshape(
-        months, 2, levels // block, block, lat_rows, lon_cells
-    )
-    weighted = jnp.moveaxis(weighted, 2, 1).reshape(turns, 2, block, lat_rows, lon_cells)
-    combined = jnp.where(
-        basin_id[None, None] > 0, (basin_id[None, None] - 1) * CLASSES + dens_class, -1
-    )
-    combined = combined.reshape(turns, block, lat_rows, lon_cells)
-    column_ids = jnp.arange(BASINS * CLASSES, dtype=jnp.int32)
-
-    def one_block(packed):
-        onehot = (packed[1][..., None] == column_ids).astype(jnp.bfloat16)
-        return jnp.einsum("skji,kjiq->sqj", packed[0], onehot, preferred_element_type=jnp.float32)
-
-    per_block = lax.map(one_block, (weighted, combined))
-    per_block = per_block.reshape(months, levels // block, 2, BASINS, CLASSES, lat_rows)
-    return jnp.swapaxes(jnp.sum(per_block, axis=1), 1, 2)
-
-
-def local_tables(north_vel, up_vel, dens_class, thickness, basin_id, first_row, lat_total):
-    months, levels, lat_rows, lon_cells = north_vel.shape
-    row_index = first_row + jnp.arange(lat_rows, dtype=jnp.int32)
-    latitude = (-78.0 + 156.0 * (row_index.astype(jnp.float32) + 0.5) / lat_total) * (
-        math.pi / 180.0
-    )
-    zonal_width = jnp.cos(latitude)
-    layer_depth = thickness.astype(jnp.float32) * 0.001
-    wet_cells = (thickness > 0).astype(jnp.float32)
-    north_flux = (
-        north_vel.astype(jnp.float32)
-        * (north_unit * zonal_width)[None, None, :, None]
-        * layer_depth[None]
-    ).astype(jnp.bfloat16)
-    rise_flux = (
-        up_vel.astype(jnp.float32) * (up_unit * zonal_width)[None, None, :, None] * wet_cells[None]
-    ).astype(jnp.bfloat16)
-    basin_masks = (
-        basin_id[None] == jnp.arange(1, BASINS + 1, dtype=jnp.int32)[:, None, None]
-    ).astype(jnp.bfloat16)
-    north_depth = jnp.einsum(
-        "mkji,bji->mbkj", north_flux, basin_masks, preferred_element_type=jnp.float32
-    )
-    rise_depth = jnp.einsum(
-        "mkji,bji->mbkj", rise_flux, basin_masks, preferred_element_type=jnp.float32
-    )
-    depth_tab = jnp.stack([north_depth, rise_depth], 2)
-    class_tab = class_sums(north_flux, rise_flux, dens_class, basin_id)
-    return (class_tab, depth_tab)
+NT = (((1,), (1,)), ((), ()))
+
+def tables_kernel(lat_axis, pairs, rounds, n_ref, u_ref, c_ref, th_ref, b_ref, t_ref, d_ref,
+                  cn_ref, cr_ref, hb_ref, mk_ref, acc_ref, f_ref):
+    levels, rows, lons = th_ref.shape
+    groups = rows // 8
+    bf = jnp.bfloat16
+    f32 = jnp.float32
+
+    @pl.when(pl.program_id(0) == 0)
+    def _():
+        first = (lax.axis_index(lat_axis) if lat_axis else 0) * rows
+        j = lax.broadcasted_iota(jnp.int32, (rows, lons), 0) + first
+        phi = (-78.0 + 156.0 * (j.astype(f32) + 0.5) / 128) * (math.pi / 180.0)
+        zw = jnp.cos(phi)
+
+        @pl.loop(0, levels)
+        def _(k):
+            th = th_ref[k]
+            cn_ref[k] = (0.02 * zw) * (th.astype(f32) * 0.001)
+            cr_ref[k] = jnp.where(th > 0, 0.01 * zw, 0.0)
+
+        for k in range(levels, cn_ref.shape[0]):
+            cn_ref[k] = jnp.zeros((rows, lons), f32)
+            cr_ref[k] = jnp.zeros((rows, lons), f32)
+        b = b_ref[...]
+        hb_ref[...] = jnp.where(b > 0, (b - 1) * 5, -100)
+        z = jnp.zeros((128, lons), bf)
+        m = jnp.concatenate([(b == v).astype(f32) for v in (1, 2, 3)] + [jnp.zeros((rows, lons), f32)], 0).astype(bf)
+        mk_ref[...] = jnp.concatenate(
+            [jnp.concatenate([m, z], 1), jnp.concatenate([z, m], 1)], 0)
+
+    zero = jnp.zeros((16, lons), bf)
+    one = jnp.ones((16, lons), bf)
+
+    def build(k, tile):
+        kk = jnp.minimum(k, levels - 1)
+        r0 = 16 * tile
+        nf = n_ref[0, kk, r0:r0 + 16, :].astype(f32) * cn_ref[k, r0:r0 + 16, :]
+        rf = u_ref[0, kk, r0:r0 + 16, :].astype(f32) * cr_ref[k, r0:r0 + 16, :]
+        cc = c_ref[0, kk, r0:r0 + 16, :]
+        hi = ((cc >> 4) + hb_ref[r0:r0 + 16, :]).astype(f32)
+        lo = (cc & 15).astype(f32)
+        out = []
+        for s in range(2):
+            a, b = nf[8 * s:8 * s + 8], rf[8 * s:8 * s + 8]
+            h, l = hi[8 * s:8 * s + 8], lo[8 * s:8 * s + 8]
+            nn = jnp.concatenate([a, a], 0).astype(bf)
+            rr = jnp.concatenate([b, b], 0).astype(bf)
+            fl = jnp.concatenate([a, b], 0).astype(bf)
+            hh = jnp.concatenate([h, h - 1.0], 0).astype(bf)
+            ll = jnp.concatenate([l, l - 1.0], 0).astype(bf)
+            S = [jnp.where(hh == bf(2 * q), one, zero) for q in range(8)]
+            ms = [ll == bf(2 * q) for q in range(8)]
+            P = [jnp.where(m, nn, zero) for m in ms] + [jnp.where(m, rr, zero) for m in ms]
+            out.append((jnp.concatenate(S, 0), jnp.concatenate(P, 0), fl))
+        return out
+
+    def chunk(base, first):
+        for tile in range(groups // 2):
+            got = [[], []]
+            for t in range(2 * pairs):
+                for s, item in enumerate(build(base + t, tile)):
+                    got[s].append(item)
+            for s in range(2):
+                g = 2 * tile + s
+                S = jnp.concatenate([x[0] for x in got[s]], 1)
+                P = jnp.concatenate([x[1] for x in got[s]], 1)
+                r = lax.dot_general(S, P, NT, preferred_element_type=f32)
+                acc_ref[g] = r if first else acc_ref[g] + r
+                for p in range(pairs):
+                    f_ref[base // 2 + p, 16 * g:16 * g + 16, :] = jnp.concatenate(
+                        [got[s][2 * p][2], got[s][2 * p + 1][2]], 1)
+
+    for g in range(groups):
+        acc_ref[g] = jnp.zeros(acc_ref.shape[1:], f32)
+
+    @pl.loop(0, rounds)
+    def _(r):
+        chunk(r * 2 * pairs, False)
+
+    i_row = lax.broadcasted_iota(jnp.int32, (8, 256), 0)
+    i_col = lax.broadcasted_iota(jnp.int32, (8, 256), 1)
+    keep = (i_col % 8) == i_row
+    for g in range(groups):
+        x = acc_ref[g].reshape(16, 8, 256)
+        t_ref[0, g] = jnp.sum(jnp.where(keep[None], x, 0.0), axis=1)
+
+    npairs = pairs * rounds
+    d_row = lax.broadcasted_iota(jnp.int32, (8, 256), 0)
+    d_col = lax.broadcasted_iota(jnp.int32, (8, 256), 1)
+
+    nb = f_ref.shape[0]
+    F = f_ref[...].reshape(nb * 16 * groups, 256)
+    R = lax.dot_general(F, mk_ref[...], NT, preferred_element_type=f32).reshape(nb, groups, 2, 8, 256)
+    tot = 0.0
+    for g in range(groups):
+        tot = tot + jnp.where((d_col % 32) == d_row + 8 * g, R[:, g], 0.0)
+    tot = jnp.sum(tot, axis=2)
+    d_ref[0] = tot
+
+
+def tables(north, up, dens, thick, basin, lat_axis=None, pairs=19, rounds=2):
+    months, levels, rows, lons = north.shape
+    groups = rows // 8
+    npairs = pairs * rounds
+    big = lambda: pl.BlockSpec((1, levels, rows, lons), lambda m: (m, 0, 0, 0))
+    return pl.pallas_call(
+        functools.partial(tables_kernel, lat_axis, pairs, rounds),
+        grid=(months,),
+        in_specs=[big(), big(), big(),
+                  pl.BlockSpec((levels, rows, lons), lambda m: (0, 0, 0), pipeline_mode=pl.Buffered(1)),
+                  pl.BlockSpec((rows, lons), lambda m: (0, 0), pipeline_mode=pl.Buffered(1))],
+        out_specs=[pl.BlockSpec((1, groups, 16, 256), lambda m: (m, 0, 0, 0)),
+                   pl.BlockSpec((1, npairs, 2, 256), lambda m: (m, 0, 0, 0))],
+        out_shape=[jax.ShapeDtypeStruct((months, groups, 16, 256), jnp.float32),
+                   jax.ShapeDtypeStruct((months, npairs, 2, 256), jnp.float32)],
+        scratch_shapes=[
+            pltpu.VMEM((2 * npairs, rows, lons), jnp.float32),
+            pltpu.VMEM((2 * npairs, rows, lons), jnp.float32),
+            pltpu.VMEM((rows, lons), jnp.int32),
+            pltpu.VMEM((256, 256), jnp.bfloat16),
+            pltpu.VMEM((groups, 128, 256), jnp.float32),
+            pltpu.VMEM((npairs, 16 * groups, 256), jnp.bfloat16),
+        ],
+        compiler_params=pltpu.CompilerParams(vmem_limit_bytes=60 * 2**20),
+        name="tables",
+    )(north, up, dens, thick, basin)
+
+def whole_tables(north_vel, up_vel, dens_class, thickness, basin_id):
+    t, d = tables(north_vel[0], up_vel[0], dens_class[0], thickness, basin_id, "lat")
+    months, groups = t.shape[:2]
+    t = t.reshape(months, groups, 16, 2, 16, 8)[:, :, :15]
+    class_tab = t.reshape(months, groups, 3, 5, 2, 16, 8).transpose(0, 2, 4, 3, 5, 1, 6)
+    class_tab = class_tab.reshape(1, months, 3, 2, 80, groups * 8)
+    levels = thickness.shape[0]
+    d = d.reshape(months, -1, 2, 2, 4, groups * 8).transpose(0, 4, 2, 1, 3, 5)
+    depth_tab = d.reshape(months, 4, 2, -1, groups * 8)[None, :, :3, :, :levels]
+    return class_tab, depth_tab
 
 
 def with_global(tables):
@@ -143,16 +229,7 @@
 
 
 def body(north_vel, up_vel, dens_class, thickness, basin_id):
-    row_count = north_vel.shape[3]
-    first_row = lax.axis_index("lat") * row_count
-    lat_total = row_count * lax.axis_size("lat")
-
-    def one_member(packed):
-        return local_tables(
-            packed[0], packed[1], packed[2], thickness, basin_id, first_row, lat_total
-        )
-
-    class_tab, depth_tab = lax.map(one_member, (north_vel, up_vel, dens_class))
+    class_tab, depth_tab = whole_tables(north_vel, up_vel, dens_class, thickness, basin_id)
     class_tab, depth_tab = in_one_piece((class_tab, depth_tab), "lon", 1, 4)
     class_reg = with_global(class_tab)
     depth_reg = with_global(depth_tab)

time: 362 us -> 122 us (0.34)
  matrix products: 213 us -> 0 us
  local copies, waits for them, and re-layouts: 49.8 us -> 14.7 us
  Pallas kernels: 0 us -> 33.5 us
  other arithmetic: 29 us -> 5.4 us
    dot_general x22 -> x0, matrix products: 213 us -> none  [the longest x20 209 us: one_block(): jnp.einsum('skji,kjiq->sqj', packed[0], onehot, preferred_element_type=jn...]
    dynamic_slice x60 -> x0, local copies, waits for them, and re-layouts: 41.6 us -> none  [class_sums(): per_block = lax.map(one_block, (weighted, combined))]
    pallas_call x0 -> x1, Pallas kernels: none -> 33.5 us  [tables(): pl.pallas_call(functools.partial(tables_kernel, lat_axis, pairs, rounds),...]
    convert_element_type x5 -> x0, other arithmetic: 9.07 us -> none  [the longest x2 4.72 us: local_tables(): north_flux = (north_vel.astype(jnp.float32) * (north_unit * zonal_width)[...]
    select_n x1 -> x0, other arithmetic: 5.42 us -> none  [class_sums(): jnp.where(basin_id[None, None] > 0, (basin_id[None, None] - 1) * CLASSES...]
    unnamed x4 -> x0, other arithmetic: 4.61 us -> none
where the time goes in v1:
time: 122 us
  blocking collectives  51.8 us (42%)
  Pallas kernels  33.5 us (27%)
  local copies, waits for them, and re-layouts  14.7 us (12%)
  waiting for transfers between devices  10.4 us (9%)
  other arithmetic  5.4 us (4%)
  starting transfers between devices  5 us (4%)
    pallas_call x1, Pallas kernels, tables(): pl.pallas_call(functools.partial(tables_kernel, lat_axis, pairs, rounds),...  33.5 us
    all_to_all x1, blocking collectives, summed_on_arrival(): lax.all_to_all(cut_along(shard, dim, devices), axis, 0, 0, tiled=True)  25.8 us
    all_to_all x1, blocking collectives, sent_to_all(): return lax.all_to_all(copies, axis, split_axis=0, concat_axis=0, tiled=True)  15.6 us
    all_gather x1, blocking collectives, in_one_piece_2(): lax.all_gather(both, axis, axis=dim, tiled=True)  10.5 us
    all_to_all x1, waiting for transfers between devices, summed_on_arrival(): lax.all_to_all(cut_along(shard, dim, devices), axis, 0, 0, tiled=True)  10.4 us
    all_to_all x1, starting transfers between devices, summed_on_arrival(): lax.all_to_all(cut_along(shard, dim, devices), axis, 0, 0, tiled=True)  5 us
    unnamed x5, local copies, waits for them, and re-layouts  3.54 us
    slice x1, local copies, waits for them, and re-layouts, whole_tables(): t = t.reshape(months, groups, 16, 2, 16, 8)[:, :, :15]  3.13 us
  transfers between devices with their start and end apart: 1, of which 1 were waited for; matrix products, arithmetic and copies ran while one was open for 0% of the time, Pallas kernels for 0%

profile of v1, /device:TPU:1, one launch (start us, length us, event | category | flops | bytes accessed | tf_op | source)
XLA Modules:
  0.0 121.8 jit_solution(3797192307862089483)
XLA Ops:
  0.6 33.5 %tables.1 = (f32[4,4,16,256]{3,2,1,0:T(8,128)}, f32[4,38,2,256]{3,2,1,0:T(2,128)}) custom-call(bf16[4,75,32,128]{3,2,1,0:T(8,128)(2,1)} %bitcast.33, bf16[4,75,32,128]{3,2,1,0:T(8,128)(2,1)} %bitcast.34, s32[4,75,32,128]{3,2,1,0:T(8,128)} %bitcast.32, s32[75,32,128]{2,1,0:T(8,128)} %th_ref.1, s32[32,128]{1,0:T(8,128)} %b_ref.1), custom_call_target="tpu_custom_call" | custom-call | tf_op jit(solution)/shard_map/tables/pallas_call | solution.py:193
  34.1 1.5 %copy.66 = f32[4,4,16,256]{2,3,1,0:T(8,128)S(1)} copy(f32[4,4,16,256]{3,2,1,0:T(8,128)} %get-tuple-element.6) | data formatting | bytes 524288 | tf_op jit(solution)/shard_map/tables/pallas_call | solution.py:193
  35.6 3.1 %copy.67 = f32[4,4,15,2,16,8]{4,5,3,2,1,0:T(8,128)} copy(f32[4,4,15,2,16,8]{2,5,4,3,1,0:T(8,128)S(1)} %bitcast.29) | data formatting | bytes 491520 | tf_op jit(solution)/shard_map/slice | solution.py:218
  38.8 2.3 %copy.68 = f32[4,3,2,5,16,4,8]{4,3,6,5,2,1,0:T(8,128)S(1)} copy(f32[4,3,2,5,16,4,8]{4,6,2,3,1,5,0:T(8,128)} %bitcast.30) | data formatting | bytes 491520 | tf_op jit(solution)/shard_map/transpose | solution.py:219
  41.1 0.5 reshape.246
  41.6 1.0 copy.69
  42.6 0.5 reshape.247
  43.2 0.3 copy.86
  43.6 1.2 maximum_bitcast_fusion
  44.7 5.0 %all-to-all-start = ((f32[4,1,1,3,2,155,32]{5,6,4,3,2,1,0:T(8,128)}), f32[4,1,1,3,2,155,32]{5,6,4,3,2,1,0:T(8,128)S(1)}, u32[]{:S(2)}, u32[]{:S(2)}) async-start(f32[4,1,1,3,2,155,32]{5,6,4,3,2,1,0:T(8,128)} %maximum_bitcast_fusion), calls=%async_computation | async-start | bytes 1572864 | tf_op jit(solution)/shard_map/all_to_all | solution.py:27
  49.7 10.4 %all-to-all-done = f32[4,1,1,3,2,155,32]{5,6,4,3,2,1,0:T(8,128)S(1)} async-done(((f32[4,1,1,3,2,155,32]{5,6,4,3,2,1,0:T(8,128)}), f32[4,1,1,3,2,155,32]{5,6,4,3,2,1,0:T(8,128)S(1)}, u32[]{:S(2)}, u32[]{:S(2)}) %all-to-all-start) | async-done | bytes 476192 | tf_op jit(solution)/shard_map/all_to_all | solution.py:27
  60.5 10.5 %all_gather.3 = f32[4,1,1,4,155]{4,3,2,1,0:T(4,128)S(1)} all-gather(f32[1,1,1,4,155]{4,3,2,1,0:T(4,128)S(1)} %pad_maximum_fusion.5), channel_id=1, replica_groups=mesh['lon'=4,'lat'=4,'mem'=16] {'lat'}, dimensions={0}, use_global_device_ids=true | all-gather | bytes 12400 | tf_op jit(solution)/shard_map/all_gather | solution.py:46
  71.2 0.9 reduce_window_sum.51
  73.0 0.9 reduce_window_sum.54
  74.5 0.4 all_to_all.14
  74.9 25.8 %all_to_all.20 = f32[16,1,4960]{2,1,0:T(1,128)S(1)} all-to-all(f32[16,1,4960]{2,1,0:T(1,128)S(1)} %all_to_all.14), channel_id=1, replica_groups=mesh['lon'=4,'lat'=4,'mem'=16] {'mem'}, dimensions={0} | all-to-all | bytes 634880 | tf_op jit(solution)/shard_map/all_to_all | solution.py:27
  100.7 0.2 reduce_sum.98
  101.1 15.6 %all_to_all.21 = f32[16,1,4960]{2,1,0:T(1,128)S(1)} all-to-all(f32[16,1,4960]{2,1,0:T(1,128)S(1)} %broadcast_in_dim.27), channel_id=1, replica_groups=mesh['lon'=4,'lat'=4,'mem'=16] {'mem'}, dimensions={0} | all-to-all | bytes 634880 | tf_op jit(solution)/shard_map/all_to_all | solution.py:58
  116.7 0.8 reduce.10
  117.4 0.2 reshape.251
  118.1 0.8 copy.81
  118.9 0.8 copy.82
  120.1 0.8 copy.79
  120.9 0.8 copy.80
  (35 shorter events, 3.1 us)
Async XLA Ops:
  44.7 15.4 %all-to-all-start = ((f32[4,1,1,3,2,155,32]{5,6,4,3,2,1,0:T(8,128)}), f32[4,1,1,3,2,155,32]{5,6,4,3,2,1,0:T(8,128)S(1)}, u32[]{:S(2)}, u32[]{:S(2)}) async-start(f32[4,1,1,3,2,155,32]{5,6,4,3,2,1,0:T(8,128)} %maximum_bitcast_fusion), calls=%async_computation | async-start | bytes 1572864 | tf_op jit(solution)/shard_map/all_to_all | solution.py:27

commit v2 on v1

v2 whole, which is shorter than its diff:
```python
import functools
import math

import jax
import jax.numpy as jnp
from jax import lax
from jax.experimental import pallas as pl
from jax.experimental.pallas import tpu as pltpu
from jax.sharding import PartitionSpec as P

NT = (((1,), (1,)), ((), ()))

def tables_kernel(lat_axis, lat_total, pairs, rounds, n_ref, u_ref, c_ref, th_ref, b_ref, t_ref, d_ref,
                  cn_ref, cr_ref, hb_ref, mk_ref, acc_ref, f_ref):
    levels, rows, lons = th_ref.shape
    groups = rows // 8
    bf = jnp.bfloat16
    f32 = jnp.float32

    @pl.when(pl.program_id(0) == 0)
    def _():
        first = (lax.axis_index(lat_axis) if lat_axis else 0) * rows
        j = lax.broadcasted_iota(jnp.int32, (rows, lons), 0) + first
        phi = (-78.0 + 156.0 * (j.astype(f32) + 0.5) / lat_total) * (math.pi / 180.0)
        zw = jnp.cos(phi)

        @pl.loop(0, levels)
        def _(k):
            th = th_ref[k]
            cn_ref[k] = (0.02 * zw) * (th.astype(f32) * 0.001)
            cr_ref[k] = jnp.where(th > 0, 0.01 * zw, 0.0)

        for k in range(levels, cn_ref.shape[0]):
            cn_ref[k] = jnp.zeros((rows, lons), f32)
            cr_ref[k] = jnp.zeros((rows, lons), f32)
        b = b_ref[...]
        hb_ref[...] = jnp.where(b > 0, (b - 1) * 5, -100)
        z = jnp.zeros((128, lons), bf)
        m = jnp.concatenate([(b == v).astype(f32) for v in (1, 2, 3)] + [jnp.zeros((128 - 3 * rows, lons), f32)], 0).astype(bf)
        mk_ref[...] = jnp.concatenate(
            [jnp.concatenate([m, z], 1), jnp.concatenate([z, m], 1)], 0)

    zero = jnp.zeros((16, lons), bf)
    one = jnp.ones((16, lons), bf)

    def build(k, tile):
        kk = jnp.minimum(k, levels - 1)
        r0 = 16 * tile
        nf = n_ref[0, kk, r0:r0 + 16, :].astype(f32) * cn_ref[k, r0:r0 + 16, :]
        rf = u_ref[0, kk, r0:r0 + 16, :].astype(f32) * cr_ref[k, r0:r0 + 16, :]
        cc = c_ref[0, kk, r0:r0 + 16, :]
        hi = ((cc >> 4) + hb_ref[r0:r0 + 16, :]).astype(f32)
        lo = (cc & 15).astype(f32)
        out = []
        for s in range(2):
            a, b = nf[8 * s:8 * s + 8], rf[8 * s:8 * s + 8]
            h, l = hi[8 * s:8 * s + 8], lo[8 * s:8 * s + 8]
            nn = jnp.concatenate([a, a], 0).astype(bf)
            rr = jnp.concatenate([b, b], 0).astype(bf)
            fl = jnp.concatenate([a, b], 0).astype(bf)
            hh = jnp.concatenate([h, h - 1.0], 0).astype(bf)
            ll = jnp.concatenate([l, l - 1.0], 0).astype(bf)
            S = [jnp.where(hh == bf(2 * q), one, zero) for q in range(8)]
            ms = [ll == bf(2 * q) for q in range(8)]
            P = [jnp.where(m, nn, zero) for m in ms] + [jnp.where(m, rr, zero) for m in ms]
            out.append((jnp.concatenate(S, 0), jnp.concatenate(P, 0), fl))
        return out

    def chunk(base, first):
        for tile in range(groups // 2):
            got = [[], []]
            for t in range(2 * pairs):
                for s, item in enumerate(build(base + t, tile)):
                    got[s].append(item)
            for s in range(2):
                g = 2 * tile + s
                S = jnp.concatenate([x[0] for x in got[s]], 1)
                P = jnp.concatenate([x[1] for x in got[s]], 1)
                r = lax.dot_general(S, P, NT, preferred_element_type=f32)
                acc_ref[g] = r if first else acc_ref[g] + r
                for p in range(pairs):
                    f_ref[base // 2 + p, 16 * g:16 * g + 16, :] = jnp.concatenate(
                        [got[s][2 * p][2], got[s][2 * p + 1][2]], 1)

    for g in range(groups):
        acc_ref[g] = jnp.zeros(acc_ref.shape[1:], f32)

    @pl.loop(0, rounds)
    def _(r):
        chunk(r * 2 * pairs, False)

    i_row = lax.broadcasted_iota(jnp.int32, (8, 256), 0)
    i_col = lax.broadcasted_iota(jnp.int32, (8, 256), 1)
    keep = (i_col % 8) == i_row
    for g in range(groups):
        x = acc_ref[g].reshape(16, 8, 256)
        t_ref[0, g] = jnp.sum(jnp.where(keep[None], x, 0.0), axis=1)

    npairs = pairs * rounds
    d_row = lax.broadcasted_iota(jnp.int32, (8, 256), 0)
    d_col = lax.broadcasted_iota(jnp.int32, (8, 256), 1)

    nb = f_ref.shape[0]
    F = f_ref[...].reshape(nb * 16 * groups, 256)
    R = lax.dot_general(F, mk_ref[...], NT, preferred_element_type=f32).reshape(nb, groups, 2, 8, 256)
    for f in range(2):
        tot = 0.0
        for g in range(groups):
            tot = tot + jnp.where((d_col % rows) == d_row + 8 * g, R[:, g, f], 0.0)
        d_ref[0, f] = jnp.sum(tot, axis=1)


def tables(north, up, dens, thick, basin, lat_axis=None, lat_total=128, pairs=19, rounds=2):
    months, levels, rows, lons = north.shape
    groups = rows // 8
    npairs = pairs * rounds
    big = lambda: pl.BlockSpec((1, levels, rows, lons), lambda m: (m, 0, 0, 0))
    return pl.pallas_call(
        functools.partial(tables_kernel, lat_axis, lat_total, pairs, rounds),
        grid=(months,),
        in_specs=[big(), big(), big(),
                  pl.BlockSpec((levels, rows, lons), lambda m: (0, 0, 0), pipeline_mode=pl.Buffered(1)),
                  pl.BlockSpec((rows, lons), lambda m: (0, 0), pipeline_mode=pl.Buffered(1))],
        out_specs=[pl.BlockSpec((1, groups, 16, 256), lambda m: (m, 0, 0, 0)),
                   pl.BlockSpec((1, 2, npairs, 256), lambda m: (m, 0, 0, 0))],
        out_shape=[jax.ShapeDtypeStruct((months, groups, 16, 256), jnp.float32),
                   jax.ShapeDtypeStruct((months, 2, npairs, 256), jnp.float32)],
        scratch_shapes=[
            pltpu.VMEM((2 * npairs, rows, lons), jnp.float32),
            pltpu.VMEM((2 * npairs, rows, lons), jnp.float32),
            pltpu.VMEM((rows, lons), jnp.int32),
            pltpu.VMEM((256, 256), jnp.bfloat16),
            pltpu.VMEM((groups, 128, 256), jnp.float32),
            pltpu.VMEM((npairs, 16 * groups, 256), jnp.bfloat16),
        ],
        compiler_params=pltpu.CompilerParams(vmem_limit_bytes=60 * 2**20),
        name="tables",
    )(north, up, dens, thick, basin)


def merge_kernel(nlon, nlat, nmem, t_ref, d_ref, dm_ref, ds_ref, cm_ref, cs_ref,
                 tb, db, pk, pb, a_ref, mine, got, res,
                 send_l, recv_l, send_x, recv_x, send_m, recv_m, send_g, recv_g):
    f32 = jnp.float32
    mesh_id = pl.DeviceIdType.MESH
    y, x, me = lax.axis_index("lon"), lax.axis_index("lat"), lax.axis_index("mem")
    groups = t_ref.shape[1]
    lat_rows = 8 * groups
    piece = 320 // nmem

    def other(axis, index):
        return dict(device_id={axis: index}, device_id_type=mesh_id)

    barrier = pltpu.get_barrier_semaphore()
    for axis, at, n in (("lon", y, nlon), ("lat", x, nlat), ("mem", me, nmem)):
        for d in range(1, n):
            pl.semaphore_signal(barrier, inc=1, **other(axis, lax.rem(at + d, n)))
    pl.semaphore_wait(barrier, nlon + nlat + nmem - 3)

    sends = []
    for d in range(1, nlon):
        p = lax.rem(y + d, nlon)
        for q, (src, dst) in enumerate(((t_ref, tb), (d_ref, db))):
            c = pltpu.make_async_remote_copy(
                src.at[p], dst.at[d - 1], send_l.at[d - 1, q], recv_l.at[d - 1, q], **other("lon", p))
            c.start()
            sends.append(c)
    lane = lax.broadcasted_iota(jnp.int32, (8, 128), 1)
    wide = lax.broadcasted_iota(jnp.int32, (80, 128), 1)
    tall = lax.broadcasted_iota(jnp.int32, (80, 128), 0)

    def down(v):
        for s in (1, 2, 4, 8, 16, 32, 64):
            v = v + jnp.where(tall >= s, pltpu.roll(v, s, 0), 0.0)
        return v

    def along(v, at):
        s = 1
        while s < lat_rows:
            v = v + jnp.where(at % lat_rows >= s, pltpu.roll(v, s, 1), 0.0)
            s *= 2
        return v

    def regions(v):
        g = pltpu.roll(v, lat_rows, 1) + pltpu.roll(v, 2 * lat_rows, 1) + pltpu.roll(v, 3 * lat_rows, 1)
        return jnp.where((wide >= 3 * lat_rows) & (wide < 4 * lat_rows), g, v)

    for c in sends:
        c.wait_recv()
    T = t_ref[y]
    D = d_ref[y]
    for d in range(nlon - 1):
        T = T + tb[d]
        D = D + db[d]

    for f in range(2):
        R = {}
        for g in range(groups):
            for b in range(3):
                v = T[g, 5 * b:5 * b + 5, 128 * f:128 * f + 128]
                v = jnp.concatenate([v, jnp.zeros((3, 128), f32)], 0)
                s = lat_rows * b + 8 * g
                R[b, g] = pltpu.roll(v, s, 1) if s else v
        for l in range(16):
            z = jnp.zeros((8, 128), f32)
            for (b, g), v in R.items():
                z = jnp.where(lane // 8 == (groups * b + g + l) % 16, v, z)
            if l:
                z = pltpu.roll(z, 128 - 8 * l, 1)
            a_ref[f, pl.ds(l, 5, stride=16), :] = z[:5]
        levels2 = D.shape[1]
        a_ref[2 + f, 72:80, :] = jnp.zeros((8, 128), f32)
        a_ref[2 + f, pl.ds(0, levels2, stride=2), :] = D[f, :, 0:128]
        a_ref[2 + f, pl.ds(1, levels2, stride=2), :] = D[f, :, 128:256]

    up = [along(regions(a_ref[1]), wide), along(regions(a_ref[3]), wide)]
    packed = jnp.zeros((8, 128), f32)
    for q in range(2):
        for v in range(10):
            r = (10 * q + v - (lat_rows - 1)) % 128
            w = up[q][8 * v:8 * v + 8]
            packed = jnp.where(lane % lat_rows == 10 * q + v, pltpu.roll(w, r, 1) if r else w, packed)
    pk[...] = packed
    sends_x = []
    for d in range(1, nlat):
        p = lax.rem(x + d, nlat)
        c = pltpu.make_async_remote_copy(
            pk, pb.at[d - 1], send_x.at[d - 1], recv_x.at[d - 1], **other("lat", p))
        c.start()
        sends_x.append(c)

    def hand_in(a, v):
        a_ref[a] = v
        for o in range(a * nmem // 4, (a + 1) * nmem // 4):
            r0 = o * piece - 80 * a
            mine[o] = a_ref[a, r0:r0 + piece, :]

    hand_in(0, down(regions(a_ref[0])))
    hand_in(2, down(regions(a_ref[2])))

    carry = jnp.zeros((8, 128), f32)
    for d, c in enumerate(sends_x):
        c.wait_recv()
        carry = carry + jnp.where(x > d, pb[d], 0.0)
    for q in range(2):
        parts = []
        for v in range(10):
            r = (-(10 * q + v)) % 128
            w = pltpu.roll(carry, r, 1) if r else carry
            parts.append(jnp.where((lane % lat_rows == 0) & (lane < 4 * lat_rows), w, 0.0))
        up[q] = up[q] + along(jnp.concatenate(parts, 0), wide)
    hand_in(1, down(up[0]))
    hand_in(3, up[1])

    sends_m = []
    for d in range(1, nmem):
        p = lax.rem(me + d, nmem)
        c = pltpu.make_async_remote_copy(
            mine.at[p], got.at[d - 1], send_m.at[d - 1], recv_m.at[d - 1], **other("mem", p))
        c.start()
        sends_m.append(c)
    own = mine[me]
    total = own
    for d, c in enumerate(sends_m):
        c.wait_recv()
        total = total + got[d]
    mean = total * (1.0 / nmem)
    square = jnp.square(own - mean)
    for d in range(nmem - 1):
        square = square + jnp.square(got[d] - mean)
    res[me, 0] = mean
    res[me, 1] = jnp.sqrt(square * (1.0 / (nmem - 1)))

    core = lax.rem(me, 2)
    partner = me + 1 - 2 * core
    sends_g = []

    def give(piece_of, to, slot):
        c = pltpu.make_async_remote_copy(
            res.at[piece_of], res.at[piece_of], send_g.at[slot], recv_g.at[piece_of], **other("mem", to))
        c.start()
        sends_g.append(c)

    def take(piece_of):
        pltpu.make_async_remote_copy(
            res.at[piece_of], res.at[piece_of], send_g.at[0], recv_g.at[piece_of], **other("mem", partner)).wait_recv()

    for d in range(2, nmem, 2):
        give(me, lax.rem(me + d, nmem), d)
    give(me, partner, 0)
    for d in range(2, nmem, 2):
        p = lax.rem(me + nmem - d, nmem)
        take(p)
        give(p, partner, d + 1)
    for d in range(0, nmem, 2):
        take(lax.rem(partner + nmem - d, nmem))

    for k, (c_out, d_out) in enumerate(((cm_ref, dm_ref), (cs_ref, ds_ref))):
        for a, out in enumerate((c_out, c_out, d_out, d_out)):
            f = a % 2
            for o in range(a * nmem // 4, (a + 1) * nmem // 4):
                r0 = o * piece - 80 * a
                a_ref[a, r0:r0 + piece, :] = res[o, k]
            v = jnp.concatenate([a_ref[a], jnp.zeros((48, 128), f32)], 0).T
            n = out.shape[-1]
            for r in range(4):
                s = lat_rows * ((r + 3) % 4)
                out[0, r, f] = v[s:s + lat_rows, :n]
    for c in sends + sends_x + sends_m + sends_g:
        c.wait_send()


def merge(t, d, levels, nlon, nlat, nmem):
    f32 = jnp.float32
    groups = t.shape[1]
    lat_rows = 8 * groups
    piece = 320 // nmem
    vm = pl.BlockSpec(memory_space=pltpu.VMEM)
    sem = pltpu.SemaphoreType.DMA
    dep = jax.ShapeDtypeStruct((1, 4, 2, lat_rows, levels), f32)
    cla = jax.ShapeDtypeStruct((1, 4, 2, lat_rows, 80), f32)
    outs = pl.pallas_call(
        functools.partial(merge_kernel, nlon, nlat, nmem),
        in_specs=[vm, vm],
        out_specs=[vm] * 4,
        out_shape=[dep, dep, cla, cla],
        scratch_shapes=[
            pltpu.VMEM((nlon - 1, *t.shape[1:]), f32),
            pltpu.VMEM((nlon - 1, *d.shape[1:]), f32),
            pltpu.VMEM((8, 128), f32),
            pltpu.VMEM((nlat - 1, 8, 128), f32),
            pltpu.VMEM((4, 80, 128), f32),
            pltpu.VMEM((nmem, piece, 128), f32),
            pltpu.VMEM((nmem - 1, piece, 128), f32),
            pltpu.VMEM((nmem, 2, piece, 128), f32),
            sem((nlon - 1, 2)), sem((nlon - 1, 2)),
            sem((nlat - 1,)), sem((nlat - 1,)),
            sem((nmem - 1,)), sem((nmem - 1,)),
            sem((nmem + 1,)), sem((nmem,)),
        ],
        compiler_params=pltpu.CompilerParams(collective_id=0, has_side_effects=True),
        name="merge",
    )(t, d)
    return tuple(jnp.swapaxes(o, 3, 4) for o in outs)


def solution(mesh):
    nlon, nlat, nmem = (mesh.shape[a] for a in ("lon", "lat", "mem"))

    def body(north_vel, up_vel, dens_class, thickness, basin_id):
        t, d = tables(
            north_vel[0], up_vel[0], dens_class[0], thickness, basin_id,
            "lat", nlat * thickness.shape[1])
        return merge(t, d, thickness.shape[0], nlon, nlat, nmem)

    big = P("mem", None, None, "lat", "lon")
    out = P("lon", None, None, None, "lat")
    return jax.shard_map(
        body, mesh=mesh, in_specs=(big, big, big, P(None, "lat", "lon"), P("lat", "lon")),
        out_specs=(out,) * 4, check_vma=False)
```

time: 122 us -> 81.9 us (0.67)
  blocking collectives: 51.8 us -> 0 us
  Pallas kernels: 33.5 us -> 74.8 us
  waiting for transfers between devices: 10.4 us -> 0 us
  local copies, waits for them, and re-layouts: 14.7 us -> 6.27 us
  other arithmetic: 5.4 us -> 0 us
  starting transfers between devices: 5 us -> 0 us
    all_to_all x2 -> x0, blocking collectives: 41.4 us -> none  [the longest x1 25.8 us: summed_on_arrival(): lax.all_to_all(cut_along(shard, dim, devices), axis, 0, 0, tiled=True)]
    pallas_call x1 -> x2, Pallas kernels: 33.5 us -> 74.8 us  [the longest x1 41.3 us: merge(): pl.pallas_call(functools.partial(merge_kernel, nlon, nlat, nmem), in_spec...]
    all_gather x1 -> x0, blocking collectives: 10.5 us -> none  [in_one_piece_2(): lax.all_gather(both, axis, axis=dim, tiled=True)]
    all_to_all x1 -> x0, waiting for transfers between devices: 10.4 us -> none  [summed_on_arrival(): lax.all_to_all(cut_along(shard, dim, devices), axis, 0, 0, tiled=True)]
    all_to_all x1 -> x0, starting transfers between devices: 5 us -> none  [summed_on_arrival(): lax.all_to_all(cut_along(shard, dim, devices), axis, 0, 0, tiled=True)]
    slice x8 -> x0, local copies, waits for them, and re-layouts: 3.7 us -> none  [the longest x1 3.13 us: whole_tables(): t = t.reshape(months, groups, 16, 2, 16, 8)[:, :, :15]]
    another operation x8 -> x0, other arithmetic: 3.45 us -> none  [the longest x1 1.16 us: cut_along(): return jnp.moveaxis(parts, dim, 0)]
    unnamed x5 -> x4, local copies, waits for them, and re-layouts: 3.54 us -> 6.27 us
  transfers between devices with their start and end apart: 1 -> 0, of which waited for: 1 -> 0; matrix products, arithmetic and copies ran while one was open for 0% -> 0% of each run, Pallas kernels for 0% -> 0%
where the time goes in v2:
time: 81.9 us; the launch traced here: 81.7 us
  Pallas kernels  74.8 us (91%)
  local copies, waits for them, and re-layouts  6.27 us (8%)
    pallas_call x1, Pallas kernels, merge(): pl.pallas_call(functools.partial(merge_kernel, nlon, nlat, nmem), in_spec...  41.3 us
    pallas_call x1, Pallas kernels, tables(): pl.pallas_call(functools.partial(tables_kernel, lat_axis, lat_total, pair...  33.5 us
    unnamed x4, local copies, waits for them, and re-layouts  6.27 us

profile of v2, /device:TPU:1, one launch (start us, length us, event | category | flops | bytes accessed | tf_op | source)
XLA Modules:
  0.0 81.7 jit_solution(15231245805376980956)
XLA Ops:
  0.6 33.5 %tables.1 = (f32[4,4,16,256]{3,2,1,0:T(8,128)}, f32[4,2,38,256]{3,2,1,0:T(8,128)}) custom-call(bf16[4,75,32,128]{3,2,1,0:T(8,128)(2,1)} %bitcast.8, bf16[4,75,32,128]{3,2,1,0:T(8,128)(2,1)} %bitcast.9, s32[4,75,32,128]{3,2,1,0:T(8,128)} %bitcast.7, s32[75,32,128]{2,1,0:T(8,128)} %th_ref.1, s32[32,128]{1,0:T(8,128)} %b_ref.1), custom_call_target="tpu_custom_call" | custom-call | tf_op jit(solution)/shard_map/tables/pallas_call | solution.py:118
  34.1 41.3 %merge.1 = (f32[1,4,2,32,75]{4,3,2,1,0:T(8,128)}, f32[1,4,2,32,75]{4,3,2,1,0:T(8,128)}, f32[1,4,2,32,80]{4,3,2,1,0:T(8,128)}, f32[1,4,2,32,80]{4,3,2,1,0:T(8,128)}) custom-call(f32[4,4,16,256]{3,2,1,0:T(8,128)} %get-tuple-element.10.t_ref, f32[4,2,38,256]{3,2,1,0:T(8,128)} %get-tuple-element.11.d_ref), custom_call_target="tpu_custom_call" | custom-call | tf_op jit(solution)/shard_map/merge/pallas_call | solution.py:322
  75.5 1.6 %copy.13 = f32[1,4,2,75,32]{3,4,2,1,0:T(8,128)} copy(f32[1,4,2,75,32]{3,4,2,1,0:T(8,128)} %bitcast.13) | data formatting | bytes 153600
  77.0 1.6 %copy.14 = f32[1,4,2,75,32]{3,4,2,1,0:T(8,128)} copy(f32[1,4,2,75,32]{3,4,2,1,0:T(8,128)} %bitcast.12) | data formatting | bytes 153600
  78.6 1.6 %copy.15 = f32[1,4,2,80,32]{3,4,2,1,0:T(8,128)} copy(f32[1,4,2,80,32]{3,4,2,1,0:T(8,128)} %bitcast.11) | data formatting | bytes 163840
  80.2 1.6 %copy.16 = f32[1,4,2,80,32]{3,4,2,1,0:T(8,128)} copy(f32[1,4,2,80,32]{3,4,2,1,0:T(8,128)} %bitcast.10) | data formatting | bytes 163840

commit v3 on v2

--- a/solution.py
+++ b/solution.py
@@ -8,14 +8,11 @@
 from jax.experimental.pallas import tpu as pltpu
 from jax.sharding import PartitionSpec as P
 
-NT = (((1,), (1,)), ((), ()))
-
 def tables_kernel(lat_axis, lat_total, pairs, rounds, n_ref, u_ref, c_ref, th_ref, b_ref, t_ref, d_ref,
-                  cn_ref, cr_ref, hb_ref, mk_ref, acc_ref, f_ref):
+                  cn_ref, cr_ref, hb_ref, mk_ref, f_ref):
     levels, rows, lons = th_ref.shape
     groups = rows // 8
-    bf = jnp.bfloat16
-    f32 = jnp.float32
+    bf, f32, f8 = jnp.bfloat16, jnp.float32, jnp.float8_e4m3fn
 
     @pl.when(pl.program_id(0) == 0)
     def _():
@@ -34,7 +31,7 @@
             cn_ref[k] = jnp.zeros((rows, lons), f32)
             cr_ref[k] = jnp.zeros((rows, lons), f32)
         b = b_ref[...]
-        hb_ref[...] = jnp.where(b > 0, (b - 1) * 5, -100)
+        hb_ref[...] = jnp.where(b > 0, (b - 1) * 10, -100)
         z = jnp.zeros((128, lons), bf)
         m = jnp.concatenate([(b == v).astype(f32) for v in (1, 2, 3)] + [jnp.zeros((128 - 3 * rows, lons), f32)], 0).astype(bf)
         mk_ref[...] = jnp.concatenate(
@@ -49,8 +46,8 @@
         nf = n_ref[0, kk, r0:r0 + 16, :].astype(f32) * cn_ref[k, r0:r0 + 16, :]
         rf = u_ref[0, kk, r0:r0 + 16, :].astype(f32) * cr_ref[k, r0:r0 + 16, :]
         cc = c_ref[0, kk, r0:r0 + 16, :]
-        hi = ((cc >> 4) + hb_ref[r0:r0 + 16, :]).astype(f32)
-        lo = (cc & 15).astype(f32)
+        hi = ((cc >> 3) + hb_ref[r0:r0 + 16, :]).astype(f32)
+        lo = (cc & 7).astype(f32)
         out = []
         for s in range(2):
             a, b = nf[8 * s:8 * s + 8], rf[8 * s:8 * s + 8]
@@ -60,54 +57,54 @@
             fl = jnp.concatenate([a, b], 0).astype(bf)
             hh = jnp.concatenate([h, h - 1.0], 0).astype(bf)
             ll = jnp.concatenate([l, l - 1.0], 0).astype(bf)
-            S = [jnp.where(hh == bf(2 * q), one, zero) for q in range(8)]
-            ms = [ll == bf(2 * q) for q in range(8)]
+            S = [jnp.where(hh == bf(2 * q), one, zero) for q in range(16)]
+            S = [jnp.concatenate(S[2 * q:2 * q + 2], 0).astype(f8) for q in range(8)]
+            ms = [ll == bf(2 * q) for q in range(4)]
             P = [jnp.where(m, nn, zero) for m in ms] + [jnp.where(m, rr, zero) for m in ms]
             out.append((jnp.concatenate(S, 0), jnp.concatenate(P, 0), fl))
         return out
 
-    def chunk(base, first):
-        for tile in range(groups // 2):
-            got = [[], []]
-            for t in range(2 * pairs):
-                for s, item in enumerate(build(base + t, tile)):
-                    got[s].append(item)
-            for s in range(2):
-                g = 2 * tile + s
-                S = jnp.concatenate([x[0] for x in got[s]], 1)
-                P = jnp.concatenate([x[1] for x in got[s]], 1)
-                r = lax.dot_general(S, P, NT, preferred_element_type=f32)
-                acc_ref[g] = r if first else acc_ref[g] + r
-                for p in range(pairs):
-                    f_ref[base // 2 + p, 16 * g:16 * g + 16, :] = jnp.concatenate(
-                        [got[s][2 * p][2], got[s][2 * p + 1][2]], 1)
-
-    for g in range(groups):
-        acc_ref[g] = jnp.zeros(acc_ref.shape[1:], f32)
-
-    @pl.loop(0, rounds)
-    def _(r):
-        chunk(r * 2 * pairs, False)
-
     i_row = lax.broadcasted_iota(jnp.int32, (8, 256), 0)
     i_col = lax.broadcasted_iota(jnp.int32, (8, 256), 1)
-    keep = (i_col % 8) == i_row
-    for g in range(groups):
-        x = acc_ref[g].reshape(16, 8, 256)
-        t_ref[0, g] = jnp.sum(jnp.where(keep[None], x, 0.0), axis=1)
-
-    npairs = pairs * rounds
-    d_row = lax.broadcasted_iota(jnp.int32, (8, 256), 0)
-    d_col = lax.broadcasted_iota(jnp.int32, (8, 256), 1)
-
-    nb = f_ref.shape[0]
-    F = f_ref[...].reshape(nb * 16 * groups, 256)
-    R = lax.dot_general(F, mk_ref[...], NT, preferred_element_type=f32).reshape(nb, groups, 2, 8, 256)
-    for f in range(2):
-        tot = 0.0
+
+    def month(accs, deps):
+        @pl.loop(0, rounds)
+        def _(r):
+            for p in range(pairs):
+                for tile in range(groups // 2):
+                    even = build(2 * (r * pairs + p), tile)
+                    odd = build(2 * (r * pairs + p) + 1, tile)
+                    for s in range(2):
+                        g = 2 * tile + s
+                        S, P, F = (jnp.concatenate([x, y], 1) for x, y in zip(even[s], odd[s]))
+                        pltpu.matmul_push_rhs(S, staging_register=tile % 2, mxu_index=s, transpose=True)
+                        pltpu.matmul_acc_lhs(accs[g], P, load_staged_rhs=tile % 2)
+                        f_ref[g, r * pairs + p] = F
+
+        for s in range(2):
+            pltpu.matmul_push_rhs(mk_ref[...], staging_register=0, mxu_index=s, transpose=True)
+        half = f_ref.shape[1] // 2
+        for h in range(2):
+            tot = [0.0, 0.0]
+            for g in range(groups):
+                pltpu.matmul_acc_lhs(
+                    deps[g], f_ref[g, half * h:half * h + half].reshape(16 * half, 256),
+                    load_staged_rhs=0 if g < 2 and h == 0 else None)
+            for g in range(groups):
+                R = pltpu.matmul_pop(deps[g]).reshape(half, 2, 8, 256)
+                for f in range(2):
+                    tot[f] = tot[f] + jnp.where((i_col % rows) == i_row + 8 * g, R[:, f], 0.0)
+            for f in range(2):
+                d_ref[0, f, half * h:half * h + half, :] = jnp.sum(tot[f], axis=1)
         for g in range(groups):
-            tot = tot + jnp.where((d_col % rows) == d_row + 8 * g, R[:, g, f], 0.0)
-        d_ref[0, f] = jnp.sum(tot, axis=1)
+            x = pltpu.matmul_pop(accs[g]).reshape(16, 8, 256)
+            t_ref[0, g] = jnp.sum(jnp.where((i_col % 8) == i_row, x, 0.0), axis=1)
+
+    half = f_ref.shape[1] // 2
+    pl.run_scoped(
+        month,
+        tuple(pltpu.ACC(g % 2)((128, 256), f32) for g in range(groups)),
+        tuple(pltpu.ACC(g % 2)((16 * half, 256), f32) for g in range(groups)))
 
 
 def tables(north, up, dens, thick, basin, lat_axis=None, lat_total=128, pairs=19, rounds=2):
@@ -130,15 +127,14 @@
             pltpu.VMEM((2 * npairs, rows, lons), jnp.float32),
             pltpu.VMEM((rows, lons), jnp.int32),
             pltpu.VMEM((256, 256), jnp.bfloat16),
-            pltpu.VMEM((groups, 128, 256), jnp.float32),
-            pltpu.VMEM((npairs, 16 * groups, 256), jnp.bfloat16),
+            pltpu.VMEM((groups, npairs, 16, 256), jnp.bfloat16),
         ],
         compiler_params=pltpu.CompilerParams(vmem_limit_bytes=60 * 2**20),
         name="tables",
     )(north, up, dens, thick, basin)
 
 
-def merge_kernel(nlon, nlat, nmem, t_ref, d_ref, dm_ref, ds_ref, cm_ref, cs_ref,
+def merge_kernel(nlon, nlat, nmem, t_ref, d_ref, all_ref,
                  tb, db, pk, pb, a_ref, mine, got, res,
                  send_l, recv_l, send_x, recv_x, send_m, recv_m, send_g, recv_g):
     f32 = jnp.float32
@@ -197,17 +193,17 @@
         R = {}
         for g in range(groups):
             for b in range(3):
-                v = T[g, 5 * b:5 * b + 5, 128 * f:128 * f + 128]
-                v = jnp.concatenate([v, jnp.zeros((3, 128), f32)], 0)
-                s = lat_rows * b + 8 * g
+                v = T[g, 8 * f:8 * f + 8, :]
+                s = (lat_rows * b + 8 * g - 80 * b) % 256
                 R[b, g] = pltpu.roll(v, s, 1) if s else v
-        for l in range(16):
+        for h in range(10):
             z = jnp.zeros((8, 128), f32)
             for (b, g), v in R.items():
-                z = jnp.where(lane // 8 == (groups * b + g + l) % 16, v, z)
-            if l:
-                z = pltpu.roll(z, 128 - 8 * l, 1)
-            a_ref[f, pl.ds(l, 5, stride=16), :] = z[:5]
+                q = groups * b + g + h
+                z = jnp.where(lane // 8 == q % 16, v[:, :128] if q < 16 else v[:, 128:], z)
+            if h:
+                z = pltpu.roll(z, 128 - 8 * h, 1)
+            a_ref[f, 8 * h:8 * h + 8, :] = z
         levels2 = D.shape[1]
         a_ref[2 + f, 72:80, :] = jnp.zeros((8, 128), f32)
         a_ref[2 + f, pl.ds(0, levels2, stride=2), :] = D[f, :, 0:128]
@@ -295,35 +291,23 @@
     for d in range(0, nmem, 2):
         take(lax.rem(partner + nmem - d, nmem))
 
-    for k, (c_out, d_out) in enumerate(((cm_ref, dm_ref), (cs_ref, ds_ref))):
-        for a, out in enumerate((c_out, c_out, d_out, d_out)):
-            f = a % 2
-            for o in range(a * nmem // 4, (a + 1) * nmem // 4):
-                r0 = o * piece - 80 * a
-                a_ref[a, r0:r0 + piece, :] = res[o, k]
-            v = jnp.concatenate([a_ref[a], jnp.zeros((48, 128), f32)], 0).T
-            n = out.shape[-1]
-            for r in range(4):
-                s = lat_rows * ((r + 3) % 4)
-                out[0, r, f] = v[s:s + lat_rows, :n]
+    all_ref[...] = res[...]
     for c in sends + sends_x + sends_m + sends_g:
         c.wait_send()
 
 
-def merge(t, d, levels, nlon, nlat, nmem):
+def merge(t, d, nlon, nlat, nmem):
     f32 = jnp.float32
     groups = t.shape[1]
     lat_rows = 8 * groups
     piece = 320 // nmem
     vm = pl.BlockSpec(memory_space=pltpu.VMEM)
     sem = pltpu.SemaphoreType.DMA
-    dep = jax.ShapeDtypeStruct((1, 4, 2, lat_rows, levels), f32)
-    cla = jax.ShapeDtypeStruct((1, 4, 2, lat_rows, 80), f32)
-    outs = pl.pallas_call(
+    return pl.pallas_call(
         functools.partial(merge_kernel, nlon, nlat, nmem),
         in_specs=[vm, vm],
-        out_specs=[vm] * 4,
-        out_shape=[dep, dep, cla, cla],
+        out_specs=vm,
+        out_shape=jax.ShapeDtypeStruct((nmem, 2, piece, 128), f32),
         scratch_shapes=[
             pltpu.VMEM((nlon - 1, *t.shape[1:]), f32),
             pltpu.VMEM((nlon - 1, *d.shape[1:]), f32),
@@ -341,6 +325,37 @@
         compiler_params=pltpu.CompilerParams(collective_id=0, has_side_effects=True),
         name="merge",
     )(t, d)
+
+
+def finish_kernel(lat_rows, all_ref, dm_ref, ds_ref, cm_ref, cs_ref, a_ref):
+    nmem, piece = all_ref.shape[0], all_ref.shape[2]
+    a_ref[...] = jnp.zeros_like(a_ref)
+    for k, outs in enumerate(((cm_ref, dm_ref), (cs_ref, ds_ref))):
+        for a in range(4):
+            for o in range(a * nmem // 4, (a + 1) * nmem // 4):
+                r0 = o * piece - 80 * a
+                a_ref[4 * k + a, r0:r0 + piece, :] = all_ref[o, k]
+        for a in range(4):
+            v = a_ref[4 * k + a].T
+            out = outs[a // 2]
+            for r in range(4):
+                s = lat_rows * ((r + 3) % 4)
+                out[0, r, a % 2] = v[s:s + lat_rows, :out.shape[-1]]
+
+
+def finish(res, levels, lat_rows):
+    f32 = jnp.float32
+    vm = pl.BlockSpec(memory_space=pltpu.VMEM)
+    dep = jax.ShapeDtypeStruct((1, 4, 2, lat_rows, levels), f32)
+    cla = jax.ShapeDtypeStruct((1, 4, 2, lat_rows, 80), f32)
+    outs = pl.pallas_call(
+        functools.partial(finish_kernel, lat_rows),
+        in_specs=[vm],
+        out_specs=[vm] * 4,
+        out_shape=[dep, dep, cla, cla],
+        scratch_shapes=[pltpu.VMEM((8, 128, 128), f32)],
+        name="finish",
+    )(res)
     return tuple(jnp.swapaxes(o, 3, 4) for o in outs)
 
 
@@ -351,7 +366,8 @@
         t, d = tables(
             north_vel[0], up_vel[0], dens_class[0], thickness, basin_id,
             "lat", nlat * thickness.shape[1])
-        return merge(t, d, thickness.shape[0], nlon, nlat, nmem)
+        res = merge(t, d, nlon, nlat, nmem)
+        return finish(res, *thickness.shape[:2])
 
     big = P("mem", None, None, "lat", "lon")
     out = P("lon", None, None, None, "lat")

time: 81.9 us -> 61.1 us (0.75)
  Pallas kernels: 74.8 us -> 60.3 us
  local copies, waits for them, and re-layouts: 6.27 us -> 0 us
    pallas_call x1, Pallas kernels: 33.5 us -> 17.8 us  [tables(): pl.pallas_call(functools.partial(tables_kernel, lat_axis, lat_total, pair...]
    unnamed x4 -> x0, local copies, waits for them, and re-layouts: 6.27 us -> none
    pallas_call x0 -> x1, Pallas kernels: none -> 1.94 us  [finish(): pl.pallas_call(functools.partial(finish_kernel, lat_rows), in_specs=[vm],...]
where the time goes in v3:
time: 61.1 us; the launch traced here: 61 us
  Pallas kernels  60.3 us (99%)
  between operations  0.64 us (1%)
    pallas_call x1, Pallas kernels, merge(): pl.pallas_call(functools.partial(merge_kernel, nlon, nlat, nmem), in_spec...  40.6 us
    pallas_call x1, Pallas kernels, tables(): pl.pallas_call(functools.partial(tables_kernel, lat_axis, lat_total, pair...  17.8 us
    pallas_call x1, Pallas kernels, finish(): pl.pallas_call(functools.partial(finish_kernel, lat_rows), in_specs=[vm],...  1.94 us

profile of v3, /device:TPU:1, one launch (start us, length us, event | category | flops | bytes accessed | tf_op | source)
XLA Modules:
  0.0 61.0 jit_solution(1791081294225518228)
XLA Ops:
  0.6 17.8 %tables.1 = (f32[4,4,16,256]{3,2,1,0:T(8,128)}, f32[4,2,38,256]{3,2,1,0:T(8,128)}) custom-call(bf16[4,75,32,128]{3,2,1,0:T(8,128)(2,1)} %bitcast.8, bf16[4,75,32,128]{3,2,1,0:T(8,128)(2,1)} %bitcast.9, s32[4,75,32,128]{3,2,1,0:T(8,128)} %bitcast.7, s32[75,32,128]{2,1,0:T(8,128)} %th_ref.1, s32[32,128]{1,0:T(8,128)} %b_ref.1), custom_call_target="tpu_custom_call" | custom-call | tf_op jit(solution)/shard_map/tables/pallas_call | solution.py:115
  18.4 40.6 %merge.1.all_ref = f32[16,2,20,128]{3,2,1,0:T(8,128)} custom-call(f32[4,4,16,256]{3,2,1,0:T(8,128)} %get-tuple-element.10.t_ref, f32[4,2,38,256]{3,2,1,0:T(8,128)} %get-tuple-element.11.d_ref), custom_call_target="tpu_custom_call" | custom-call | tf_op jit(solution)/shard_map/merge/pallas_call | solution.py:306
  59.0 1.9 %finish.1 = (f32[1,4,2,32,75]{4,3,2,1,0:T(8,128)}, f32[1,4,2,32,75]{4,3,2,1,0:T(8,128)}, f32[1,4,2,32,80]{4,3,2,1,0:T(8,128)}, f32[1,4,2,32,80]{4,3,2,1,0:T(8,128)}) custom-call(f32[16,2,20,128]{3,2,1,0:T(8,128)} %merge.1.all_ref), custom_call_target="tpu_custom_call" | custom-call | tf_op jit(solution)/shard_map/finish/pallas_call | solution.py:351

commit v4 on v3

v4 whole, which is shorter than its diff:
```python
import functools
import math

import jax
import jax.numpy as jnp
from jax import lax
from jax.experimental import pallas as pl
from jax.experimental.pallas import tpu as pltpu
from jax.sharding import PartitionSpec as P

MESH = pl.DeviceIdType.MESH
PIECE = 320
UNROLL = 19


def build(n_ref, u_ref, c_ref, cn_ref, cr_ref, hb_ref, slot, k, tile):
    bf, f32, f8 = jnp.bfloat16, jnp.float32, jnp.float8_e4m3fn
    r0 = 16 * tile
    nf = n_ref[slot, k, r0:r0 + 16, :].astype(f32) * cn_ref[k, r0:r0 + 16, :]
    rf = u_ref[slot, k, r0:r0 + 16, :].astype(f32) * cr_ref[k, r0:r0 + 16, :]
    cc = c_ref[slot, k, r0:r0 + 16, :]
    hi = ((cc >> 3) + hb_ref[r0:r0 + 16, :]).astype(f32)
    lo = (cc & 7).astype(f32)
    zero = jnp.zeros((16, cc.shape[1]), bf)
    one = jnp.ones((16, cc.shape[1]), bf)
    out = []
    for s in range(2):
        a, b = nf[8 * s:8 * s + 8], rf[8 * s:8 * s + 8]
        h, l = hi[8 * s:8 * s + 8], lo[8 * s:8 * s + 8]
        nn = jnp.concatenate([a, a], 0).astype(bf)
        rr = jnp.concatenate([b, b], 0).astype(bf)
        fl = jnp.concatenate([a, b], 0).astype(bf)
        hh = jnp.concatenate([h, h - 1.0], 0).astype(bf)
        ll = jnp.concatenate([l, l - 1.0], 0).astype(bf)
        S = [jnp.where(hh == bf(2 * q), one, zero) for q in range(16)]
        S = [jnp.concatenate(S[2 * q:2 * q + 2], 0).astype(f8) for q in range(8)]
        ms = [ll == bf(2 * q) for q in range(4)]
        V = [jnp.where(m, nn, zero) for m in ms] + [jnp.where(m, rr, zero) for m in ms]
        out.append((jnp.concatenate(S, 0), jnp.concatenate(V, 0), fl))
    return out


def kernel(nlon, nlat, nmem, n_hbm, u_hbm, c_hbm, th_hbm, b_ref, all_ref,
           n_buf, u_buf, c_buf, th_ref, cn_ref, cr_ref, hb_ref, mk_ref, f_ref,
           t_ref, d_ref, tb, db, pk, pb, a_ref, mine, got, res,
           in_sem, th_sem, send_l, recv_l, send_x, recv_x, send_m, recv_m, send_g, recv_g):
    bf, f32 = jnp.bfloat16, jnp.float32
    y, x, me = lax.axis_index("lon"), lax.axis_index("lat"), lax.axis_index("mem")
    months, levels, rows, lons = n_hbm.shape
    groups = rows // 8
    padded = cn_ref.shape[0]
    npairs = padded // 2
    half = npairs // 2
    rounds = npairs // UNROLL
    nz = nmem // 2
    piece = PIECE // nmem

    def other(axis, index):
        return dict(device_id={axis: index}, device_id_type=MESH)

    barrier = pltpu.get_barrier_semaphore()
    for axis, at, n in (("lon", y, nlon), ("lat", x, nlat), ("mem", me, nmem)):
        for d in range(1, n):
            pl.semaphore_signal(barrier, inc=1, **other(axis, lax.rem(at + d, n)))

    def inputs(s):
        month, slot = lax.rem(y + 1 + s, months), lax.rem(s, 2)
        return [pltpu.make_async_copy(src.at[month], buf.at[slot, pl.ds(0, levels)], in_sem.at[slot, q])
                for q, (src, buf) in enumerate(((n_hbm, n_buf), (u_hbm, u_buf), (c_hbm, c_buf)))]

    th_copy = pltpu.make_async_copy(th_hbm, th_ref, th_sem)
    th_copy.start()
    for c in inputs(0):
        c.start()
    for slot in range(2):
        for k in range(levels, padded):
            n_buf[slot, k] = jnp.zeros((rows, lons), bf)
            u_buf[slot, k] = jnp.zeros((rows, lons), bf)
            c_buf[slot, k] = jnp.zeros((rows, lons), jnp.int32)
    for k in range(levels, padded):
        cn_ref[k] = jnp.zeros((rows, lons), f32)
        cr_ref[k] = jnp.zeros((rows, lons), f32)
    b = b_ref[...]
    hb_ref[...] = jnp.where(b > 0, (b - 1) * 10, -100)
    z = jnp.zeros((128, lons), bf)
    m = jnp.concatenate([(b == v).astype(f32) for v in (1, 2, 3)]
                        + [jnp.zeros((128 - 3 * rows, lons), f32)], 0).astype(bf)
    mk_ref[...] = jnp.concatenate([jnp.concatenate([m, z], 1), jnp.concatenate([z, m], 1)], 0)
    j = lax.broadcasted_iota(jnp.int32, (rows, lons), 0) + x * rows
    phi = (-78.0 + 156.0 * (j.astype(f32) + 0.5) / (rows * nlat)) * (math.pi / 180.0)
    zw = jnp.cos(phi)
    zn, zr = 0.02 * zw, 0.01 * zw
    th_copy.wait()

    @pl.loop(0, levels // 5)
    def _(q):
        for k in range(5):
            th = th_ref[5 * q + k]
            cn_ref[5 * q + k] = zn * (th.astype(f32) * 0.001)
            cr_ref[5 * q + k] = jnp.where(th > 0, zr, 0.0)

    for k in range(levels // 5 * 5, levels):
        th = th_ref[k]
        cn_ref[k] = zn * (th.astype(f32) * 0.001)
        cr_ref[k] = jnp.where(th > 0, zr, 0.0)

    i_row = lax.broadcasted_iota(jnp.int32, (8, 256), 0)
    i_col = lax.broadcasted_iota(jnp.int32, (8, 256), 1)

    def to_owner(s):
        p = lax.rem(y + 1 + s, nlon)
        return [pltpu.make_async_remote_copy(
            src.at[s], dst.at[s], send_l.at[s, q], recv_l.at[s, q], **other("lon", p))
            for q, (src, dst) in enumerate(((t_ref, tb), (d_ref, db)))]

    def tables(accs, deps):
        @pl.loop(0, months)
        def _(s):
            slot = lax.rem(s, 2)
            for c in inputs(s):
                c.wait()

            @pl.when(s < months - 1)
            def _():
                for c in inputs(s + 1):
                    c.start()

            @pl.loop(0, rounds)
            def _(r):
                for p in range(UNROLL):
                    for tile in range(groups // 2):
                        even, odd = (build(n_buf, u_buf, c_buf, cn_ref, cr_ref, hb_ref,
                                           slot, 2 * (r * UNROLL + p) + e, tile) for e in range(2))
                        for q in range(2):
                            g = 2 * tile + q
                            S, V, F = (jnp.concatenate([v, w], 1) for v, w in zip(even[q], odd[q]))
                            pltpu.matmul_push_rhs(S, staging_register=tile % 2, mxu_index=q, transpose=True)
                            pltpu.matmul_acc_lhs(accs[g], V, load_staged_rhs=tile % 2)
                            f_ref[g, r * UNROLL + p] = F

            for q in range(2):
                pltpu.matmul_push_rhs(mk_ref[...], staging_register=0, mxu_index=q, transpose=True)
            for g in range(groups):
                v = pltpu.matmul_pop(accs[g]).reshape(16, 8, 256)
                t_ref[s, g] = jnp.sum(jnp.where((i_col % 8) == i_row, v, 0.0), axis=1)
            for h in range(2):
                tot = [0.0, 0.0]
                for g in range(groups):
                    pltpu.matmul_acc_lhs(
                        deps[g], f_ref[g, half * h:half * h + half].reshape(16 * half, 256),
                        load_staged_rhs=0 if g < 2 and h == 0 else None)
                for g in range(groups):
                    R = pltpu.matmul_pop(deps[g]).reshape(half, 2, 8, 256)
                    for f in range(2):
                        tot[f] = tot[f] + jnp.where((i_col % rows) == i_row + 8 * g, R[:, f], 0.0)
                for f in range(2):
                    d_ref[s, f, half * h:half * h + half, :] = jnp.sum(tot[f], axis=1)

            @pl.when(s == 0)
            def _():
                pl.semaphore_wait(barrier, nlon + nlat + nmem - 3)

            @pl.when(s < months - 1)
            def _():
                for c in to_owner(s):
                    c.start()

    pl.run_scoped(
        tables,
        tuple(pltpu.ACC(g % 2)((128, 256), f32) for g in range(groups)),
        tuple(pltpu.ACC(g % 2)((16 * half, 256), f32) for g in range(groups)))

    lane = lax.broadcasted_iota(jnp.int32, (8, 128), 1)
    wide = lax.broadcasted_iota(jnp.int32, (80, 128), 1)
    tall = lax.broadcasted_iota(jnp.int32, (80, 128), 0)

    def down(v):
        for s in (1, 2, 4, 8, 16, 32, 64):
            v = v + jnp.where(tall >= s, pltpu.roll(v, s, 0), 0.0)
        return v

    def along(v):
        s = 1
        while s < rows:
            v = v + jnp.where(wide % rows >= s, pltpu.roll(v, s, 1), 0.0)
            s *= 2
        return v

    def regions(v):
        w = pltpu.roll(v, rows, 1) + pltpu.roll(v, 2 * rows, 1) + pltpu.roll(v, 3 * rows, 1)
        return jnp.where((wide >= 3 * rows) & (wide < 4 * rows), w, v)

    sends_l = [c for s in range(months - 1) for c in to_owner(s)]
    for c in sends_l:
        c.wait_recv()

    def class_rows(f):
        R = {}
        for g in range(groups):
            T = t_ref[months - 1, g, 8 * f:8 * f + 8, :]
            for d in range(months - 1):
                T = T + tb[d, g, 8 * f:8 * f + 8, :]
            for q in range(3):
                s = (rows * q + 8 * g - 80 * q) % 256
                R[q, g] = pltpu.roll(T, s, 1) if s else T
        for h in range(10):
            z = jnp.zeros((8, 128), f32)
            for (q, g), v in R.items():
                o = groups * q + g + h
                z = jnp.where(lane // 8 == o % 16, v[:, :128] if o < 16 else v[:, 128:], z)
            a_ref[f, 8 * h:8 * h + 8, :] = pltpu.roll(z, 128 - 8 * h, 1) if h else z
        return regions(a_ref[f])

    def depth_rows(f):
        D = d_ref[months - 1, f]
        for d in range(months - 1):
            D = D + db[d, f]
        a_ref[2 + f, 72:80, :] = jnp.zeros((8, 128), f32)
        a_ref[2 + f, pl.ds(0, npairs, stride=2), :] = D[:, 0:128]
        a_ref[2 + f, pl.ds(1, npairs, stride=2), :] = D[:, 128:256]
        return regions(a_ref[2 + f])

    up = [along(class_rows(1)), along(depth_rows(1))]
    packed = jnp.zeros((8, 128), f32)
    for q in range(2):
        for v in range(10):
            r = (10 * q + v - (rows - 1)) % 128
            w = up[q][8 * v:8 * v + 8]
            packed = jnp.where(lane % rows == 10 * q + v, pltpu.roll(w, r, 1) if r else w, packed)
    pk[...] = packed
    sends_x = []
    for d in range(1, nlat):
        c = pltpu.make_async_remote_copy(
            pk, pb.at[d - 1], send_x.at[d - 1], recv_x.at[d - 1], **other("lat", lax.rem(x + d, nlat)))
        c.start()
        sends_x.append(c)

    core = lax.rem(me, 2)
    zz = (me - core) // 2
    far_first = sorted(range(1, nz), key=lambda d: (-min(d, nz - d), d))
    sends_m = []

    def piece_to(f, dz):
        to = 2 * lax.rem(zz + dz, nz) + f
        d = lax.rem(to - me + nmem, nmem)
        return pltpu.make_async_remote_copy(
            mine.at[to], got.at[d - 1], send_m.at[d - 1], recv_m.at[d - 1], **other("mem", to))

    def hand_in(f, tables_f):
        for q, v in enumerate(tables_f):
            a_ref[2 * q + f] = v
            for t in range(nz // 2):
                mine[2 * (q * (nz // 2) + t) + f] = a_ref[2 * q + f, piece * t:piece * t + piece, :]
        for dz in far_first:
            c = piece_to(f, dz)
            c.start()
            sends_m.append(c)

        @pl.when(core != f)
        def _():
            piece_to(f, 0).start()

    hand_in(0, [down(class_rows(0)), down(depth_rows(0))])

    carry = jnp.zeros((8, 128), f32)
    for d, c in enumerate(sends_x):
        c.wait_recv()
        carry = carry + jnp.where(x > d, pb[d], 0.0)
    for q in range(2):
        parts = []
        for v in range(10):
            r = (-(10 * q + v)) % 128
            w = pltpu.roll(carry, r, 1) if r else carry
            parts.append(jnp.where((lane % rows == 0) & (lane < 4 * rows), w, 0.0))
        up[q] = up[q] + along(jnp.concatenate(parts, 0))
    hand_in(1, [down(up[0]), up[1]])

    own = mine[me]
    total = own
    for d in range(1, nmem):
        pltpu.make_async_remote_copy(
            mine.at[me], got.at[d - 1], send_m.at[d - 1], recv_m.at[d - 1],
            **other("mem", lax.rem(me + d, nmem))).wait_recv()
        total = total + got[d - 1]
    mean = total * (1.0 / nmem)
    square = jnp.square(own - mean)
    for d in range(nmem - 1):
        square = square + jnp.square(got[d] - mean)
    res[me, 0] = mean
    res[me, 1] = jnp.sqrt(square * (1.0 / (nmem - 1)))

    partner = me + 1 - 2 * core
    sends_g = []

    def give(piece_of, to, slot):
        c = pltpu.make_async_remote_copy(
            res.at[piece_of], res.at[piece_of], send_g.at[slot], recv_g.at[piece_of], **other("mem", to))
        c.start()
        sends_g.append(c)

    def take(piece_of):
        pltpu.make_async_remote_copy(
            res.at[piece_of], res.at[piece_of], send_g.at[0], recv_g.at[piece_of], **other("mem", partner)).wait_recv()

    for dz in far_first:
        give(me, lax.rem(me + 2 * dz, nmem), 2 * dz)
    give(me, partner, 0)
    for dz in reversed(far_first):
        p = lax.rem(me + nmem - 2 * dz, nmem)
        take(p)
        give(p, partner, 2 * dz + 1)
    take(partner)
    for dz in reversed(far_first):
        take(lax.rem(partner + nmem - 2 * dz, nmem))

    all_ref[...] = res[...]
    for c in sends_l + sends_x + sends_g:
        c.wait_send()
    for d in range(1, nmem):
        pltpu.make_async_remote_copy(
            mine.at[me], got.at[d - 1], send_m.at[d - 1], recv_m.at[d - 1],
            **other("mem", lax.rem(me + d, nmem))).wait_send()


def statistics(north, up, dens, thick, basin, nlon, nlat, nmem):
    f32, bf, i32 = jnp.float32, jnp.bfloat16, jnp.int32
    months, levels, rows, lons = north.shape
    groups = rows // 8
    npairs = UNROLL * -(-levels // (2 * UNROLL))
    padded = 2 * npairs
    piece = PIECE // nmem
    vm = pl.BlockSpec(memory_space=pltpu.VMEM)
    hbm = pl.BlockSpec(memory_space=pl.ANY)
    sem = pltpu.SemaphoreType.DMA
    return pl.pallas_call(
        functools.partial(kernel, nlon, nlat, nmem),
        in_specs=[hbm, hbm, hbm, hbm, vm],
        out_specs=vm,
        out_shape=jax.ShapeDtypeStruct((nmem, 2, piece, 128), f32),
        scratch_shapes=[
            pltpu.VMEM((2, padded, rows, lons), bf),
            pltpu.VMEM((2, padded, rows, lons), bf),
            pltpu.VMEM((2, padded, rows, lons), i32),
            pltpu.VMEM((levels, rows, lons), i32),
            pltpu.VMEM((padded, rows, lons), f32),
            pltpu.VMEM((padded, rows, lons), f32),
            pltpu.VMEM((rows, lons), i32),
            pltpu.VMEM((256, 256), bf),
            pltpu.VMEM((groups, npairs, 16, 256), bf),
            pltpu.VMEM((months, groups, 16, 256), f32),
            pltpu.VMEM((months, 2, npairs, 256), f32),
            pltpu.VMEM((months - 1, groups, 16, 256), f32),
            pltpu.VMEM((months - 1, 2, npairs, 256), f32),
            pltpu.VMEM((8, 128), f32),
            pltpu.VMEM((nlat - 1, 8, 128), f32),
            pltpu.VMEM((4, 80, 128), f32),
            pltpu.VMEM((nmem, piece, 128), f32),
            pltpu.VMEM((nmem - 1, piece, 128), f32),
            pltpu.VMEM((nmem, 2, piece, 128), f32),
            sem((2, 3)), sem,
            sem((months - 1, 2)), sem((months - 1, 2)),
            sem((nlat - 1,)), sem((nlat - 1,)),
            sem((nmem - 1,)), sem((nmem - 1,)),
            sem((nmem,)), sem((nmem,)),
        ],
        compiler_params=pltpu.CompilerParams(
            collective_id=0, has_side_effects=True, vmem_limit_bytes=63 * 2**20),
        name="statistics",
    )(north, up, dens, thick, basin)


def finish_kernel(rows, all_ref, dm_ref, ds_ref, cm_ref, cs_ref, a_ref):
    nmem, piece = all_ref.shape[0], all_ref.shape[2]
    share = nmem // 4
    a_ref[...] = jnp.zeros_like(a_ref)
    for k, outs in enumerate(((cm_ref, dm_ref), (cs_ref, ds_ref))):
        for a in range(4):
            for t in range(share):
                o = 2 * (a // 2 * share + t) + a % 2
                a_ref[4 * k + a, piece * t:piece * t + piece, :] = all_ref[o, k]
        for a in range(4):
            v = a_ref[4 * k + a].T
            out = outs[a // 2]
            for r in range(4):
                s = rows * ((r + 3) % 4)
                out[0, r, a % 2] = v[s:s + rows, :out.shape[-1]]


def finish(res, levels, rows):
    f32 = jnp.float32
    vm = pl.BlockSpec(memory_space=pltpu.VMEM)
    dep = jax.ShapeDtypeStruct((1, 4, 2, rows, levels), f32)
    cla = jax.ShapeDtypeStruct((1, 4, 2, rows, 80), f32)
    outs = pl.pallas_call(
        functools.partial(finish_kernel, rows),
        in_specs=[vm],
        out_specs=[vm] * 4,
        out_shape=[dep, dep, cla, cla],
        scratch_shapes=[pltpu.VMEM((8, 128, 128), f32)],
        name="finish",
    )(res)
    return tuple(jnp.swapaxes(o, 3, 4) for o in outs)


def solution(mesh):
    nlon, nlat, nmem = (mesh.shape[a] for a in ("lon", "lat", "mem"))

    def body(north_vel, up_vel, dens_class, thickness, basin_id):
        res = statistics(north_vel[0], up_vel[0], dens_class[0], thickness, basin_id, nlon, nlat, nmem)
        return finish(res, *thickness.shape[:2])

    big = P("mem", None, None, "lat", "lon")
    out = P("lon", None, None, None, "lat")
    return jax.shard_map(
        body, mesh=mesh, in_specs=(big, big, big, P(None, "lat", "lon"), P("lat", "lon")),
        out_specs=(out,) * 4, check_vma=False)
```

time: 61.1 us -> 43.3 us (0.71)
  Pallas kernels: 60.3 us -> 42.5 us
    pallas_call x3 -> x2, Pallas kernels: 60.3 us -> 42.5 us  [the longest x1 40.5 us: statistics(): pl.pallas_call(functools.partial(kernel, nlon, nlat, nmem), in_specs=[hbm...]
where the time goes in v4:
time: 43.3 us; the launch traced here: 43.1 us
  Pallas kernels  42.5 us (98%)
  between operations  0.64 us (1%)
    pallas_call x1, Pallas kernels, statistics(): pl.pallas_call(functools.partial(kernel, nlon, nlat, nmem), in_specs=[hbm...  40.5 us
    pallas_call x1, Pallas kernels, finish(): pl.pallas_call(functools.partial(finish_kernel, rows), in_specs=[vm], out...  1.94 us

profile of v4, /device:TPU:1, one launch (start us, length us, event | category | flops | bytes accessed | tf_op | source)
XLA Modules:
  0.0 43.1 jit_solution(5466882156716448164)
XLA Ops:
  0.6 40.5 %statistics.1.all_ref = f32[16,2,20,128]{3,2,1,0:T(8,128)} custom-call(bf16[4,75,32,128]{3,2,1,0:T(8,128)(2,1)} %bitcast.8, bf16[4,75,32,128]{3,2,1,0:T(8,128)(2,1)} %bitcast.9, s32[4,75,32,128]{3,2,1,0:T(8,128)} %bitcast.7, s32[75,32,128]{2,1,0:T(8,128)} %th_hbm.1, s32[32,128]{1,0:T(8,128)} %b_ref.1), custom_call_target="tpu_custom_call" | custom-call | tf_op jit(solution)/shard_map/statistics/pallas_call | solution.py:335
  41.2 1.9 %finish.1 = (f32[1,4,2,32,75]{4,3,2,1,0:T(8,128)}, f32[1,4,2,32,75]{4,3,2,1,0:T(8,128)}, f32[1,4,2,32,80]{4,3,2,1,0:T(8,128)}, f32[1,4,2,32,80]{4,3,2,1,0:T(8,128)}) custom-call(f32[16,2,20,128]{3,2,1,0:T(8,128)} %statistics.1.all_ref), custom_call_target="tpu_custom_call" | custom-call | tf_op jit(solution)/shard_map/finish/pallas_call | solution.py:394

commit v5 on v4

--- a/solution.py
+++ b/solution.py
@@ -9,7 +9,6 @@
 from jax.sharding import PartitionSpec as P
 
 MESH = pl.DeviceIdType.MESH
-PIECE = 320
 UNROLL = 19
 
 
@@ -42,8 +41,8 @@
 
 def kernel(nlon, nlat, nmem, n_hbm, u_hbm, c_hbm, th_hbm, b_ref, all_ref,
            n_buf, u_buf, c_buf, th_ref, cn_ref, cr_ref, hb_ref, mk_ref, f_ref,
-           t_ref, d_ref, tb, db, pk, pb, a_ref, mine, got, res,
-           in_sem, th_sem, send_l, recv_l, send_x, recv_x, send_m, recv_m, send_g, recv_g):
+           t_ref, d_ref, tb, db, pk, pb, a_ref, mine, got, all_m, cs, cb, res,
+           in_sem, th_sem, send_l, recv_l, send_x, recv_x, send_m, recv_m, send_c, recv_c, send_g, recv_g):
     bf, f32 = jnp.bfloat16, jnp.float32
     y, x, me = lax.axis_index("lon"), lax.axis_index("lat"), lax.axis_index("mem")
     months, levels, rows, lons = n_hbm.shape
@@ -53,59 +52,64 @@
     half = npairs // 2
     rounds = npairs // UNROLL
     nz = nmem // 2
-    piece = PIECE // nmem
+    per = 80 // nz
+    piece = 2 * per
 
     def other(axis, index):
         return dict(device_id={axis: index}, device_id_type=MESH)
 
+    chunk = 2 * UNROLL
+    chunks = [(r, chunk * r, min(chunk, levels - chunk * r)) for r in range(rounds)]
+
+    def inputs(s, r, k0, n):
+        month, slot = lax.rem(y + 1 + s, months), lax.rem(s, 2)
+        return [pltpu.make_async_copy(
+            src.at[month, pl.ds(k0, n)], buf.at[slot, pl.ds(k0, n)], in_sem.at[slot, r, q])
+            for q, (src, buf) in enumerate(((n_hbm, n_buf), (u_hbm, u_buf), (c_hbm, c_buf)))]
+
+    def thick(r, k0, n):
+        return pltpu.make_async_copy(th_hbm.at[pl.ds(k0, n)], th_ref.at[pl.ds(k0, n)], th_sem.at[r])
+
+    for at in chunks:
+        thick(*at).start()
+        for c in inputs(0, *at):
+            c.start()
     barrier = pltpu.get_barrier_semaphore()
     for axis, at, n in (("lon", y, nlon), ("lat", x, nlat), ("mem", me, nmem)):
         for d in range(1, n):
             pl.semaphore_signal(barrier, inc=1, **other(axis, lax.rem(at + d, n)))
 
-    def inputs(s):
-        month, slot = lax.rem(y + 1 + s, months), lax.rem(s, 2)
-        return [pltpu.make_async_copy(src.at[month], buf.at[slot, pl.ds(0, levels)], in_sem.at[slot, q])
-                for q, (src, buf) in enumerate(((n_hbm, n_buf), (u_hbm, u_buf), (c_hbm, c_buf)))]
-
-    th_copy = pltpu.make_async_copy(th_hbm, th_ref, th_sem)
-    th_copy.start()
-    for c in inputs(0):
-        c.start()
     for slot in range(2):
         for k in range(levels, padded):
             n_buf[slot, k] = jnp.zeros((rows, lons), bf)
             u_buf[slot, k] = jnp.zeros((rows, lons), bf)
             c_buf[slot, k] = jnp.zeros((rows, lons), jnp.int32)
     for k in range(levels, padded):
-        cn_ref[k] = jnp.zeros((rows, lons), f32)
-        cr_ref[k] = jnp.zeros((rows, lons), f32)
+        th_ref[k] = jnp.zeros((rows, lons), jnp.int32)
     b = b_ref[...]
     hb_ref[...] = jnp.where(b > 0, (b - 1) * 10, -100)
-    z = jnp.zeros((128, lons), bf)
+    z = jnp.zeros((128, lons), f32)
     m = jnp.concatenate([(b == v).astype(f32) for v in (1, 2, 3)]
-                        + [jnp.zeros((128 - 3 * rows, lons), f32)], 0).astype(bf)
-    mk_ref[...] = jnp.concatenate([jnp.concatenate([m, z], 1), jnp.concatenate([z, m], 1)], 0)
+                        + [jnp.zeros((128 - 3 * rows, lons), f32)], 0)
+    m_row = lax.broadcasted_iota(jnp.int32, (128, lons), 0)
+    for g in range(groups):
+        mg = jnp.where(m_row % rows // 8 == g, m, 0.0)
+        mk_ref[g] = jnp.concatenate(
+            [jnp.concatenate([mg, z], 1), jnp.concatenate([z, mg], 1)], 0).astype(mk_ref.dtype)
     j = lax.broadcasted_iota(jnp.int32, (rows, lons), 0) + x * rows
     phi = (-78.0 + 156.0 * (j.astype(f32) + 0.5) / (rows * nlat)) * (math.pi / 180.0)
     zw = jnp.cos(phi)
     zn, zr = 0.02 * zw, 0.01 * zw
-    th_copy.wait()
-
-    @pl.loop(0, levels // 5)
-    def _(q):
-        for k in range(5):
-            th = th_ref[5 * q + k]
-            cn_ref[5 * q + k] = zn * (th.astype(f32) * 0.001)
-            cr_ref[5 * q + k] = jnp.where(th > 0, zr, 0.0)
-
-    for k in range(levels // 5 * 5, levels):
-        th = th_ref[k]
-        cn_ref[k] = zn * (th.astype(f32) * 0.001)
-        cr_ref[k] = jnp.where(th > 0, zr, 0.0)
 
     i_row = lax.broadcasted_iota(jnp.int32, (8, 256), 0)
     i_col = lax.broadcasted_iota(jnp.int32, (8, 256), 1)
+
+    def diagonal(v):
+        v = [jnp.where(i_col % 8 == i_row, w, 0.0) for w in v]
+        for n in (1, 2, 4):
+            low = i_row & n == 0
+            v = [jnp.where(low, p, q) + pltpu.roll(jnp.where(low, q, p), 8 - n, 0) for p, q in zip(v[::2], v[1::2])]
+        return v[0]
 
     def to_owner(s):
         p = lax.rem(y + 1 + s, nlon)
@@ -117,16 +121,34 @@
         @pl.loop(0, months)
         def _(s):
             slot = lax.rem(s, 2)
-            for c in inputs(s):
-                c.wait()
-
             @pl.when(s < months - 1)
             def _():
-                for c in inputs(s + 1):
-                    c.start()
+                for at in chunks:
+                    for c in inputs(s + 1, *at):
+                        c.start()
 
             @pl.loop(0, rounds)
             def _(r):
+                for at in chunks:
+                    @pl.when(r == at[0])
+                    def _():
+                        for c in inputs(s, *at):
+                            c.wait()
+
+                    @pl.when((r == at[0]) & (s == 0))
+                    def _():
+                        thick(*at).wait()
+
+                @pl.when(s == 0)
+                def _():
+                    @pl.loop(0, chunk // 2)
+                    def _(q):
+                        for e in range(2):
+                            k = r * chunk + 2 * q + e
+                            th = th_ref[k]
+                            cn_ref[k] = zn * (th.astype(f32) * 0.001)
+                            cr_ref[k] = jnp.where(th > 0, zr, 0.0)
+
                 for p in range(UNROLL):
                     for tile in range(groups // 2):
                         even, odd = (build(n_buf, u_buf, c_buf, cn_ref, cr_ref, hb_ref,
@@ -138,23 +160,23 @@
                             pltpu.matmul_acc_lhs(accs[g], V, load_staged_rhs=tile % 2)
                             f_ref[g, r * UNROLL + p] = F
 
+            for g in range(groups):
+                for q in range(2):
+                    pltpu.matmul_push_rhs(mk_ref[g], staging_register=g % 2, mxu_index=q, transpose=True)
+                    pltpu.matmul_acc_lhs(
+                        deps[q], f_ref[g, half * q:half * q + half].reshape(16 * half, 256), load_staged_rhs=g % 2)
+            for g in range(groups):
+                v = pltpu.matmul_pop(accs[g])
+                for f in range(2):
+                    t_ref[s, g, 8 * f:8 * f + 8, :] = diagonal(
+                        [v[64 * f + 8 * l:64 * f + 8 * l + 8] for l in range(8)])
             for q in range(2):
-                pltpu.matmul_push_rhs(mk_ref[...], staging_register=0, mxu_index=q, transpose=True)
-            for g in range(groups):
-                v = pltpu.matmul_pop(accs[g]).reshape(16, 8, 256)
-                t_ref[s, g] = jnp.sum(jnp.where((i_col % 8) == i_row, v, 0.0), axis=1)
-            for h in range(2):
-                tot = [0.0, 0.0]
-                for g in range(groups):
-                    pltpu.matmul_acc_lhs(
-                        deps[g], f_ref[g, half * h:half * h + half].reshape(16 * half, 256),
-                        load_staged_rhs=0 if g < 2 and h == 0 else None)
-                for g in range(groups):
-                    R = pltpu.matmul_pop(deps[g]).reshape(half, 2, 8, 256)
-                    for f in range(2):
-                        tot[f] = tot[f] + jnp.where((i_col % rows) == i_row + 8 * g, R[:, f], 0.0)
+                v = pltpu.matmul_pop(deps[q])
                 for f in range(2):
-                    d_ref[s, f, half * h:half * h + half, :] = jnp.sum(tot[f], axis=1)
+                    for t in range(0, half, 8):
+                        d_ref[s, f, q, t:t + 8, :] = diagonal(
+                            [v[16 * p + 8 * f:16 * p + 8 * f + 8] if p < half else jnp.zeros((8, 256), f32)
+                             for p in range(t, t + 8)])
 
             @pl.when(s == 0)
             def _():
@@ -168,7 +190,7 @@
     pl.run_scoped(
         tables,
         tuple(pltpu.ACC(g % 2)((128, 256), f32) for g in range(groups)),
-        tuple(pltpu.ACC(g % 2)((16 * half, 256), f32) for g in range(groups)))
+        tuple(pltpu.ACC(q)((16 * half, 256), f32) for q in range(2)))
 
     lane = lax.broadcasted_iota(jnp.int32, (8, 128), 1)
     wide = lax.broadcasted_iota(jnp.int32, (80, 128), 1)
@@ -216,11 +238,12 @@
         for d in range(months - 1):
             D = D + db[d, f]
         a_ref[2 + f, 72:80, :] = jnp.zeros((8, 128), f32)
-        a_ref[2 + f, pl.ds(0, npairs, stride=2), :] = D[:, 0:128]
-        a_ref[2 + f, pl.ds(1, npairs, stride=2), :] = D[:, 128:256]
+        for q in range(2):
+            for e in range(2):
+                a_ref[2 + f, pl.ds(2 * half * q + e, half, stride=2), :] = D[q, :half, 128 * e:128 * e + 128]
         return regions(a_ref[2 + f])
 
-    up = [along(class_rows(1)), along(depth_rows(1))]
+    up = [down(along(class_rows(1))), along(depth_rows(1))]
     packed = jnp.zeros((8, 128), f32)
     for q in range(2):
         for v in range(10):
@@ -249,8 +272,9 @@
     def hand_in(f, tables_f):
         for q, v in enumerate(tables_f):
             a_ref[2 * q + f] = v
-            for t in range(nz // 2):
-                mine[2 * (q * (nz // 2) + t) + f] = a_ref[2 * q + f, piece * t:piece * t + piece, :]
+        for t in range(nz):
+            mine[2 * t + f] = jnp.concatenate(
+                [a_ref[2 * q + f, pl.ds(t, per, stride=nz), :] for q in range(2)], 0)
         for dz in far_first:
             c = piece_to(f, dz)
             c.start()
@@ -260,32 +284,65 @@
         def _():
             piece_to(f, 0).start()
 
+    hand_in(1, up)
     hand_in(0, [down(class_rows(0)), down(depth_rows(0))])
 
     carry = jnp.zeros((8, 128), f32)
     for d, c in enumerate(sends_x):
         c.wait_recv()
         carry = carry + jnp.where(x > d, pb[d], 0.0)
-    for q in range(2):
-        parts = []
-        for v in range(10):
-            r = (-(10 * q + v)) % 128
-            w = pltpu.roll(carry, r, 1) if r else carry
-            parts.append(jnp.where((lane % rows == 0) & (lane < 4 * rows), w, 0.0))
-        up[q] = up[q] + along(jnp.concatenate(parts, 0))
-    hand_in(1, [down(up[0]), up[1]])
-
-    own = mine[me]
-    total = own
+    for t in range(nz):
+        cs[t] = carry[t:t + 1]
+
+    def carry_to(dz):
+        to = 2 * lax.rem(zz + dz, nz) + 1
+        d = lax.rem(to - me + nmem, nmem)
+        return pltpu.make_async_remote_copy(
+            cs.at[lax.rem(zz + dz, nz)], cb.at[d - 1], send_c.at[d - 1], recv_c.at[d - 1], **other("mem", to))
+
+    for dz in far_first:
+        carry_to(dz).start()
+
+    @pl.when(core == 0)
+    def _():
+        carry_to(0).start()
+
+    p_row = lax.broadcasted_iota(jnp.int32, (piece, 128), 0)
+    p_lane = lax.broadcasted_iota(jnp.int32, (piece, 128), 1)
+
+    def spread_out(row):
+        w = jnp.where(p_lane % rows == p_row, jnp.broadcast_to(row, (piece, 128)), 0.0)
+        n = 1
+        while n < rows:
+            w = w + jnp.where(p_lane % rows >= n, pltpu.roll(w, n, 1), pltpu.roll(w, 128 - rows + n, 1))
+            n *= 2
+        return w
+
     for d in range(1, nmem):
         pltpu.make_async_remote_copy(
             mine.at[me], got.at[d - 1], send_m.at[d - 1], recv_m.at[d - 1],
             **other("mem", lax.rem(me + d, nmem))).wait_recv()
-        total = total + got[d - 1]
+    all_m[0] = mine[me]
+    for d in range(1, nmem):
+        all_m[d] = got[d - 1]
+
+    @pl.when(core == 1)
+    def _():
+        all_m[0] = all_m[0] + spread_out(cs[zz])
+        for d in range(1, nmem):
+            pltpu.make_async_remote_copy(
+                cs.at[0], cb.at[d - 1], send_c.at[d - 1], recv_c.at[d - 1],
+                **other("mem", lax.rem(me + d, nmem))).wait_recv()
+        for d in range(1, nmem):
+            all_m[d] = all_m[d] + spread_out(cb[d - 1])
+
+    total = all_m[0]
+    for d in range(1, nmem):
+        total = total + all_m[d]
     mean = total * (1.0 / nmem)
-    square = jnp.square(own - mean)
-    for d in range(nmem - 1):
-        square = square + jnp.square(got[d] - mean)
+    square = jnp.square(all_m[0] - mean)
+    for d in range(1, nmem):
+        square = square + jnp.square(all_m[d] - mean)
     res[me, 0] = mean
     res[me, 1] = jnp.sqrt(square * (1.0 / (nmem - 1)))
 
@@ -316,6 +373,13 @@
     all_ref[...] = res[...]
     for c in sends_l + sends_x + sends_g:
         c.wait_send()
+    for dz in far_first:
+        carry_to(dz).wait_send()
+
+    @pl.when(core == 0)
+    def _():
+        carry_to(0).wait_send()
+
     for d in range(1, nmem):
         pltpu.make_async_remote_copy(
             mine.at[me], got.at[d - 1], send_m.at[d - 1], recv_m.at[d - 1],
@@ -328,7 +392,7 @@
     groups = rows // 8
     npairs = UNROLL * -(-levels // (2 * UNROLL))
     padded = 2 * npairs
-    piece = PIECE // nmem
+    piece = 320 // nmem
     vm = pl.BlockSpec(memory_space=pltpu.VMEM)
     hbm = pl.BlockSpec(memory_space=pl.ANY)
     sem = pltpu.SemaphoreType.DMA
@@ -341,25 +405,29 @@
             pltpu.VMEM((2, padded, rows, lons), bf),
             pltpu.VMEM((2, padded, rows, lons), bf),
             pltpu.VMEM((2, padded, rows, lons), i32),
-            pltpu.VMEM((levels, rows, lons), i32),
+            pltpu.VMEM((padded, rows, lons), i32),
             pltpu.VMEM((padded, rows, lons), f32),
             pltpu.VMEM((padded, rows, lons), f32),
             pltpu.VMEM((rows, lons), i32),
-            pltpu.VMEM((256, 256), bf),
+            pltpu.VMEM((groups, 256, 256), jnp.float8_e4m3fn),
             pltpu.VMEM((groups, npairs, 16, 256), bf),
             pltpu.VMEM((months, groups, 16, 256), f32),
-            pltpu.VMEM((months, 2, npairs, 256), f32),
+            pltpu.VMEM((months, 2, 2, -(-(npairs // 2) // 8) * 8, 256), f32),
             pltpu.VMEM((months - 1, groups, 16, 256), f32),
-            pltpu.VMEM((months - 1, 2, npairs, 256), f32),
+            pltpu.VMEM((months - 1, 2, 2, -(-(npairs // 2) // 8) * 8, 256), f32),
             pltpu.VMEM((8, 128), f32),
             pltpu.VMEM((nlat - 1, 8, 128), f32),
-            pltpu.VMEM((4, 80, 128), f32),
+            pltpu.VMEM((5, 80, 128), f32),
             pltpu.VMEM((nmem, piece, 128), f32),
             pltpu.VMEM((nmem - 1, piece, 128), f32),
+            pltpu.VMEM((nmem, piece, 128), f32),
+            pltpu.VMEM((nmem // 2, 1, 128), f32),
+            pltpu.VMEM((nmem - 1, 1, 128), f32),
             pltpu.VMEM((nmem, 2, piece, 128), f32),
-            sem((2, 3)), sem,
+            sem((2, npairs // UNROLL, 3)), sem((npairs // UNROLL,)),
             sem((months - 1, 2)), sem((months - 1, 2)),
             sem((nlat - 1,)), sem((nlat - 1,)),
+            sem((nmem - 1,)), sem((nmem - 1,)),
             sem((nmem - 1,)), sem((nmem - 1,)),
             sem((nmem,)), sem((nmem,)),
         ],
@@ -371,13 +439,13 @@
 
 def finish_kernel(rows, all_ref, dm_ref, ds_ref, cm_ref, cs_ref, a_ref):
     nmem, piece = all_ref.shape[0], all_ref.shape[2]
-    share = nmem // 4
+    nz, per = nmem // 2, piece // 2
     a_ref[...] = jnp.zeros_like(a_ref)
     for k, outs in enumerate(((cm_ref, dm_ref), (cs_ref, ds_ref))):
         for a in range(4):
-            for t in range(share):
-                o = 2 * (a // 2 * share + t) + a % 2
-                a_ref[4 * k + a, piece * t:piece * t + piece, :] = all_ref[o, k]
+            for t in range(nz):
+                v = all_ref[2 * t + a % 2, k]
+                a_ref[4 * k + a, pl.ds(t, per, stride=nz), :] = v[per * (a // 2):per * (a // 2 + 1)]
         for a in range(4):
             v = a_ref[4 * k + a].T
             out = outs[a // 2]

time: 43.3 us -> 44 us (1.016)
  Pallas kernels: 42.5 us -> 43.2 us
    pallas_call x1, Pallas kernels: 40.5 us -> 41.2 us  [statistics(): pl.pallas_call(functools.partial(kernel, nlon, nlat, nmem), in_specs=[hbm...]
where the time goes in v5:
time: 44 us; the launch traced here: 43.8 us
  Pallas kernels  43.2 us (98%)
  between operations  0.64 us (1%)
    pallas_call x1, Pallas kernels, statistics(): pl.pallas_call(functools.partial(kernel, nlon, nlat, nmem), in_specs=[hbm...  41.2 us
    pallas_call x1, Pallas kernels, finish(): pl.pallas_call(functools.partial(finish_kernel, rows), in_specs=[vm], out...  1.97 us

profile of v5, /device:TPU:1, one launch (start us, length us, event | category | flops | bytes accessed | tf_op | source)
XLA Modules:
  0.0 43.8 jit_solution(6441607160614982911)
XLA Ops:
  0.6 41.2 %statistics.1.all_ref = f32[16,2,20,128]{3,2,1,0:T(8,128)} custom-call(bf16[4,75,32,128]{3,2,1,0:T(8,128)(2,1)} %bitcast.8, bf16[4,75,32,128]{3,2,1,0:T(8,128)(2,1)} %bitcast.9, s32[4,75,32,128]{3,2,1,0:T(8,128)} %bitcast.7, s32[75,32,128]{2,1,0:T(8,128)} %th_hbm.1, s32[32,128]{1,0:T(8,128)} %b_ref.1), custom_call_target="tpu_custom_call" | custom-call | tf_op jit(solution)/shard_map/statistics/pallas_call | solution.py:399
  41.8 2.0 %finish.1 = (f32[1,4,2,32,75]{4,3,2,1,0:T(8,128)}, f32[1,4,2,32,75]{4,3,2,1,0:T(8,128)}, f32[1,4,2,32,80]{4,3,2,1,0:T(8,128)}, f32[1,4,2,32,80]{4,3,2,1,0:T(8,128)}) custom-call(f32[16,2,20,128]{3,2,1,0:T(8,128)} %statistics.1.all_ref), custom_call_target="tpu_custom_call" | custom-call | tf_op jit(solution)/shard_map/finish/pallas_call | solution.py:462

commit v6 on v5

--- a/solution.py
+++ b/solution.py
@@ -9,7 +9,7 @@
 from jax.sharding import PartitionSpec as P
 
 MESH = pl.DeviceIdType.MESH
-UNROLL = 19
+UNROLL = 10
 
 
 def build(n_ref, u_ref, c_ref, cn_ref, cr_ref, hb_ref, slot, k, tile):
@@ -41,7 +41,7 @@
 
 def kernel(nlon, nlat, nmem, n_hbm, u_hbm, c_hbm, th_hbm, b_ref, all_ref,
            n_buf, u_buf, c_buf, th_ref, cn_ref, cr_ref, hb_ref, mk_ref, f_ref,
-           t_ref, d_ref, tb, db, pk, pb, a_ref, mine, got, all_m, cs, cb, res,
+           t_ref, d_ref, tb, db, pk, pb, a_ref, mine, got, cs, cb, res,
            in_sem, th_sem, send_l, recv_l, send_x, recv_x, send_m, recv_m, send_c, recv_c, send_g, recv_g):
     bf, f32 = jnp.bfloat16, jnp.float32
     y, x, me = lax.axis_index("lon"), lax.axis_index("lat"), lax.axis_index("mem")
@@ -76,8 +76,10 @@
             c.start()
     barrier = pltpu.get_barrier_semaphore()
     for axis, at, n in (("lon", y, nlon), ("lat", x, nlat), ("mem", me, nmem)):
-        for d in range(1, n):
+        @pl.loop(1, n)
+        def _(d):
             pl.semaphore_signal(barrier, inc=1, **other(axis, lax.rem(at + d, n)))
+
 
     for slot in range(2):
         for k in range(levels, padded):
@@ -121,12 +123,6 @@
         @pl.loop(0, months)
         def _(s):
             slot = lax.rem(s, 2)
-            @pl.when(s < months - 1)
-            def _():
-                for at in chunks:
-                    for c in inputs(s + 1, *at):
-                        c.start()
-
             @pl.loop(0, rounds)
             def _(r):
                 for at in chunks:
@@ -138,6 +134,12 @@
                     @pl.when((r == at[0]) & (s == 0))
                     def _():
                         thick(*at).wait()
+
+                @pl.when((r == 1) & (s < months - 1))
+                def _():
+                    for at in chunks:
+                        for c in inputs(s + 1, *at):
+                            c.start()
 
                 @pl.when(s == 0)
                 def _():
@@ -260,14 +262,15 @@
 
     core = lax.rem(me, 2)
     zz = (me - core) // 2
-    far_first = sorted(range(1, nz), key=lambda d: (-min(d, nz - d), d))
-    sends_m = []
+
+    def far_first(k):
+        return nz // 2 + (k + 1) // 2 * (1 - 2 * lax.rem(k, 2))
 
     def piece_to(f, dz):
         to = 2 * lax.rem(zz + dz, nz) + f
         d = lax.rem(to - me + nmem, nmem)
         return pltpu.make_async_remote_copy(
-            mine.at[to], got.at[d - 1], send_m.at[d - 1], recv_m.at[d - 1], **other("mem", to))
+            mine.at[to], got.at[d], send_m.at[d - 1], recv_m.at[d - 1], **other("mem", to))
 
     def hand_in(f, tables_f):
         for q, v in enumerate(tables_f):
@@ -275,10 +278,9 @@
         for t in range(nz):
             mine[2 * t + f] = jnp.concatenate(
                 [a_ref[2 * q + f, pl.ds(t, per, stride=nz), :] for q in range(2)], 0)
-        for dz in far_first:
-            c = piece_to(f, dz)
-            c.start()
-            sends_m.append(c)
+        @pl.loop(0, nz - 1)
+        def _(k):
+            piece_to(f, far_first(k)).start()
 
         @pl.when(core != f)
         def _():
@@ -300,7 +302,8 @@
         return pltpu.make_async_remote_copy(
             cs.at[lax.rem(zz + dz, nz)], cb.at[d - 1], send_c.at[d - 1], recv_c.at[d - 1], **other("mem", to))
 
-    for dz in far_first:
+    @pl.loop(1, nz)
+    def _(dz):
         carry_to(dz).start()
 
     @pl.when(core == 0)
@@ -318,72 +321,94 @@
             n *= 2
         return w
 
-    for d in range(1, nmem):
-        pltpu.make_async_remote_copy(
-            mine.at[me], got.at[d - 1], send_m.at[d - 1], recv_m.at[d - 1],
-            **other("mem", lax.rem(me + d, nmem))).wait_recv()
-    all_m[0] = mine[me]
-    for d in range(1, nmem):
-        all_m[d] = got[d - 1]
+    def piece_from(d):
+        return pltpu.make_async_remote_copy(
+            mine.at[me], got.at[d], send_m.at[d - 1], recv_m.at[d - 1], **other("mem", lax.rem(me + d, nmem)))
+
+    def carry_from(d):
+        return pltpu.make_async_remote_copy(
+            cs.at[0], cb.at[d - 1], send_c.at[d - 1], recv_c.at[d - 1], **other("mem", lax.rem(me + d, nmem)))
+
+    got[0] = mine[me]
+
+    @pl.loop(1, nmem)
+    def _(d):
+        piece_from(d).wait_recv()
 
     @pl.when(core == 1)
     def _():
-        all_m[0] = all_m[0] + spread_out(cs[zz])
-        for d in range(1, nmem):
-            pltpu.make_async_remote_copy(
-                cs.at[0], cb.at[d - 1], send_c.at[d - 1], recv_c.at[d - 1],
-                **other("mem", lax.rem(me + d, nmem))).wait_recv()
-        for d in range(1, nmem):
-            all_m[d] = all_m[d] + spread_out(cb[d - 1])
-
-    total = all_m[0]
+        got[0] = got[0] + spread_out(cs[zz])
+
+        @pl.loop(1, nmem)
+        def _(d):
+            carry_from(d).wait_recv()
+
+        @pl.loop(0, (nmem - 1) // 3)
+        def _(q):
+            for e in range(3):
+                d = 3 * q + e + 1
+                got[d] = got[d] + spread_out(cb[d - 1])
+
+    total = got[0]
     for d in range(1, nmem):
-        total = total + all_m[d]
+        total = total + got[d]
     mean = total * (1.0 / nmem)
-    square = jnp.square(all_m[0] - mean)
+    square = jnp.square(got[0] - mean)
     for d in range(1, nmem):
-        square = square + jnp.square(all_m[d] - mean)
+        square = square + jnp.square(got[d] - mean)
     res[me, 0] = mean
     res[me, 1] = jnp.sqrt(square * (1.0 / (nmem - 1)))
 
     partner = me + 1 - 2 * core
-    sends_g = []
 
     def give(piece_of, to, slot):
-        c = pltpu.make_async_remote_copy(
+        return pltpu.make_async_remote_copy(
             res.at[piece_of], res.at[piece_of], send_g.at[slot], recv_g.at[piece_of], **other("mem", to))
-        c.start()
-        sends_g.append(c)
-
-    def take(piece_of):
-        pltpu.make_async_remote_copy(
-            res.at[piece_of], res.at[piece_of], send_g.at[0], recv_g.at[piece_of], **other("mem", partner)).wait_recv()
-
-    for dz in far_first:
-        give(me, lax.rem(me + 2 * dz, nmem), 2 * dz)
-    give(me, partner, 0)
-    for dz in reversed(far_first):
-        p = lax.rem(me + nmem - 2 * dz, nmem)
-        take(p)
-        give(p, partner, 2 * dz + 1)
-    take(partner)
-    for dz in reversed(far_first):
-        take(lax.rem(partner + nmem - 2 * dz, nmem))
-
-    all_ref[...] = res[...]
-    for c in sends_l + sends_x + sends_g:
-        c.wait_send()
-    for dz in far_first:
+
+    def give_far(dz):
+        return give(me, lax.rem(me + 2 * dz, nmem), 2 * dz)
+
+    def pass_on(dz):
+        return give(lax.rem(me + nmem - 2 * dz, nmem), partner, 2 * dz + 1)
+
+    @pl.loop(0, nz - 1)
+    def _(k):
+        give_far(far_first(k)).start()
+
+    give(me, partner, 0).start()
+
+    @pl.loop(1, nmem)
+    def _(d):
+        piece_from(d).wait_send()
+
+    @pl.loop(1, nz)
+    def _(dz):
         carry_to(dz).wait_send()
 
     @pl.when(core == 0)
     def _():
         carry_to(0).wait_send()
 
-    for d in range(1, nmem):
-        pltpu.make_async_remote_copy(
-            mine.at[me], got.at[d - 1], send_m.at[d - 1], recv_m.at[d - 1],
-            **other("mem", lax.rem(me + d, nmem))).wait_send()
+    for c in sends_l + sends_x:
+        c.wait_send()
+
+    @pl.loop(0, nz - 1)
+    def _(k):
+        dz = far_first(nz - 2 - k)
+        give(lax.rem(me + nmem - 2 * dz, nmem), partner, 0).wait_recv()
+        pass_on(dz).start()
+
+    @pl.loop(0, nz)
+    def _(k):
+        give(lax.rem(partner + 2 * k, nmem), partner, 0).wait_recv()
+
+    all_ref[...] = res[...]
+    @pl.loop(1, nz)
+    def _(dz):
+        give_far(dz).wait_send()
+        pass_on(dz).wait_send()
+
+    give(me, partner, 0).wait_send()
 
 
 def statistics(north, up, dens, thick, basin, nlon, nlat, nmem):
@@ -419,7 +444,6 @@
             pltpu.VMEM((nlat - 1, 8, 128), f32),
             pltpu.VMEM((5, 80, 128), f32),
             pltpu.VMEM((nmem, piece, 128), f32),
-            pltpu.VMEM((nmem - 1, piece, 128), f32),
             pltpu.VMEM((nmem, piece, 128), f32),
             pltpu.VMEM((nmem // 2, 1, 128), f32),
             pltpu.VMEM((nmem - 1, 1, 128), f32),

time: 44 us -> 46.2 us (1.050)
  Pallas kernels: 43.2 us -> 45.4 us
    pallas_call x1, Pallas kernels: 41.2 us -> 43.4 us  [statistics(): pl.pallas_call(functools.partial(kernel, nlon, nlat, nmem), in_specs=[hbm...]
where the time goes in v6:
time: 46.2 us; the launch traced here: 46 us
  Pallas kernels  45.4 us (98%)
  between operations  0.64 us (1%)
    pallas_call x1, Pallas kernels, statistics(): pl.pallas_call(functools.partial(kernel, nlon, nlat, nmem), in_specs=[hbm...  43.4 us
    pallas_call x1, Pallas kernels, finish(): pl.pallas_call(functools.partial(finish_kernel, rows), in_specs=[vm], out...  1.97 us

profile of v6, /device:TPU:1, one launch (start us, length us, event | category | flops | bytes accessed | tf_op | source)
XLA Modules:
  0.0 46.0 jit_solution(13926466858758672835)
XLA Ops:
  0.6 43.4 %statistics.1.all_ref = f32[16,2,20,128]{3,2,1,0:T(8,128)} custom-call(bf16[4,75,32,128]{3,2,1,0:T(8,128)(2,1)} %bitcast.8, bf16[4,75,32,128]{3,2,1,0:T(8,128)(2,1)} %bitcast.9, s32[4,75,32,128]{3,2,1,0:T(8,128)} %bitcast.7, s32[75,32,128]{2,1,0:T(8,128)} %th_hbm.1, s32[32,128]{1,0:T(8,128)} %b_ref.1), custom_call_target="tpu_custom_call" | custom-call | tf_op jit(solution)/shard_map/statistics/pallas_call | solution.py:424
  44.1 2.0 %finish.1 = (f32[1,4,2,32,75]{4,3,2,1,0:T(8,128)}, f32[1,4,2,32,75]{4,3,2,1,0:T(8,128)}, f32[1,4,2,32,80]{4,3,2,1,0:T(8,128)}, f32[1,4,2,32,80]{4,3,2,1,0:T(8,128)}) custom-call(f32[16,2,20,128]{3,2,1,0:T(8,128)} %statistics.1.all_ref), custom_call_target="tpu_custom_call" | custom-call | tf_op jit(solution)/shard_map/finish/pallas_call | solution.py:486

commit v7 on v4

--- a/solution.py
+++ b/solution.py
@@ -58,20 +58,21 @@
     def other(axis, index):
         return dict(device_id={axis: index}, device_id_type=MESH)
 
+    def inputs(s):
+        month, slot = lax.rem(y + 1 + s, months), lax.rem(s, 2)
+        return [pltpu.make_async_copy(src.at[month], buf.at[slot, pl.ds(0, levels)], in_sem.at[slot, q])
+                for q, (src, buf) in enumerate(((n_hbm, n_buf), (u_hbm, u_buf), (c_hbm, c_buf)))]
+
+    th_copy = pltpu.make_async_copy(th_hbm, th_ref, th_sem)
+    th_copy.start()
+    for c in inputs(0):
+        c.start()
+
     barrier = pltpu.get_barrier_semaphore()
     for axis, at, n in (("lon", y, nlon), ("lat", x, nlat), ("mem", me, nmem)):
         for d in range(1, n):
             pl.semaphore_signal(barrier, inc=1, **other(axis, lax.rem(at + d, n)))
 
-    def inputs(s):
-        month, slot = lax.rem(y + 1 + s, months), lax.rem(s, 2)
-        return [pltpu.make_async_copy(src.at[month], buf.at[slot, pl.ds(0, levels)], in_sem.at[slot, q])
-                for q, (src, buf) in enumerate(((n_hbm, n_buf), (u_hbm, u_buf), (c_hbm, c_buf)))]
-
-    th_copy = pltpu.make_async_copy(th_hbm, th_ref, th_sem)
-    th_copy.start()
-    for c in inputs(0):
-        c.start()
     for slot in range(2):
         for k in range(levels, padded):
             n_buf[slot, k] = jnp.zeros((rows, lons), bf)
@@ -107,6 +108,13 @@
     i_row = lax.broadcasted_iota(jnp.int32, (8, 256), 0)
     i_col = lax.broadcasted_iota(jnp.int32, (8, 256), 1)
 
+    def diagonal(v):
+        v = [jnp.where(i_col % 8 == i_row, w, 0.0) for w in v]
+        for n in (1, 2, 4):
+            low = i_row & n == 0
+            v = [jnp.where(low, p, q) + pltpu.roll(jnp.where(low, q, p), 8 - n, 0) for p, q in zip(v[::2], v[1::2])]
+        return v[0]
+
     def to_owner(s):
         p = lax.rem(y + 1 + s, nlon)
         return [pltpu.make_async_remote_copy(
@@ -141,8 +149,10 @@
             for q in range(2):
                 pltpu.matmul_push_rhs(mk_ref[...], staging_register=0, mxu_index=q, transpose=True)
             for g in range(groups):
-                v = pltpu.matmul_pop(accs[g]).reshape(16, 8, 256)
-                t_ref[s, g] = jnp.sum(jnp.where((i_col % 8) == i_row, v, 0.0), axis=1)
+                v = pltpu.matmul_pop(accs[g])
+                for f in range(2):
+                    t_ref[s, g, 8 * f:8 * f + 8, :] = diagonal(
+                        [v[64 * f + 8 * l:64 * f + 8 * l + 8] for l in range(8)])
             for h in range(2):
                 tot = [0.0, 0.0]
                 for g in range(groups):
@@ -305,6 +315,12 @@
     for dz in far_first:
         give(me, lax.rem(me + 2 * dz, nmem), 2 * dz)
     give(me, partner, 0)
+    for c in sends_l + sends_x:
+        c.wait_send()
+    for d in range(1, nmem):
+        pltpu.make_async_remote_copy(
+            mine.at[me], got.at[d - 1], send_m.at[d - 1], recv_m.at[d - 1],
+            **other("mem", lax.rem(me + d, nmem))).wait_send()
     for dz in reversed(far_first):
         p = lax.rem(me + nmem - 2 * dz, nmem)
         take(p)
@@ -314,12 +330,8 @@
         take(lax.rem(partner + nmem - 2 * dz, nmem))
 
     all_ref[...] = res[...]
-    for c in sends_l + sends_x + sends_g:
+    for c in sends_g:
         c.wait_send()
-    for d in range(1, nmem):
-        pltpu.make_async_remote_copy(
-            mine.at[me], got.at[d - 1], send_m.at[d - 1], recv_m.at[d - 1],
-            **other("mem", lax.rem(me + d, nmem))).wait_send()
 
 
 def statistics(north, up, dens, thick, basin, nlon, nlat, nmem):
@@ -353,7 +365,7 @@
             pltpu.VMEM((months - 1, 2, npairs, 256), f32),
             pltpu.VMEM((8, 128), f32),
             pltpu.VMEM((nlat - 1, 8, 128), f32),
-            pltpu.VMEM((4, 80, 128), f32),
+            pltpu.VMEM((5, 80, 128), f32),
             pltpu.VMEM((nmem, piece, 128), f32),
             pltpu.VMEM((nmem - 1, piece, 128), f32),
             pltpu.VMEM((nmem, 2, piece, 128), f32),

time: 43.3 us -> 43 us (level)
  no operation moved by 1% of the time
where the time goes in v7:
time: 43 us; the launch traced here: 42.8 us
  Pallas kernels  42.2 us (98%)
  between operations  0.64 us (1%)
    pallas_call x1, Pallas kernels, statistics(): pl.pallas_call(functools.partial(kernel, nlon, nlat, nmem), in_specs=[hbm...  40.2 us
    pallas_call x1, Pallas kernels, finish(): pl.pallas_call(functools.partial(finish_kernel, rows), in_specs=[vm], out...  1.94 us

profile of v7, /device:TPU:1, one launch (start us, length us, event | category | flops | bytes accessed | tf_op | source)
XLA Modules:
  0.0 42.8 jit_solution(14439578707076051610)
XLA Ops:
  0.6 40.2 %statistics.1.all_ref = f32[16,2,20,128]{3,2,1,0:T(8,128)} custom-call(bf16[4,75,32,128]{3,2,1,0:T(8,128)(2,1)} %bitcast.8, bf16[4,75,32,128]{3,2,1,0:T(8,128)(2,1)} %bitcast.9, s32[4,75,32,128]{3,2,1,0:T(8,128)} %bitcast.7, s32[75,32,128]{2,1,0:T(8,128)} %th_hbm.1, s32[32,128]{1,0:T(8,128)} %b_ref.1), custom_call_target="tpu_custom_call" | custom-call | tf_op jit(solution)/shard_map/statistics/pallas_call | solution.py:347
  40.9 1.9 %finish.1 = (f32[1,4,2,32,75]{4,3,2,1,0:T(8,128)}, f32[1,4,2,32,75]{4,3,2,1,0:T(8,128)}, f32[1,4,2,32,80]{4,3,2,1,0:T(8,128)}, f32[1,4,2,32,80]{4,3,2,1,0:T(8,128)}) custom-call(f32[16,2,20,128]{3,2,1,0:T(8,128)} %statistics.1.all_ref), custom_call_target="tpu_custom_call" | custom-call | tf_op jit(solution)/shard_map/finish/pallas_call | solution.py:406
